TPU v7x, 512 devices: a 4x2x32 block of a 4x8x32 slice. The times are simulated.
512 devices in a mesh: grp: 2 (over y), sp: 128 (over x, z), ch: 2 (over core).
Axes of the slice: x: 4, y: 2, z: 32, core: 2. Of those that a mesh axis runs over, the one named last changes fastest.
The devices are a block of a 4x8x32 slice.
Arguments:
- latents: bfloat16 [262144, 1024], P(('grp', 'sp')), parts along dimension 0, may hold values from -6 to 6
- spectrum: bfloat16 [16, 64, 128, 1024], P(None, None, 'sp', 'ch'), may hold values from -4 to 4
- w_value: bfloat16 [1024, 1024], P('sp', 'ch'), may hold values from -0.1875 to 0.1875
- w_gate: bfloat16 [1024, 1024], P('sp', 'ch'), may hold values from -0.1875 to 0.1875
- w_out: bfloat16 [1024, 1024], P('sp'), may hold values from -0.1875 to 0.1875
- embed_table: bfloat16 [1024, 32768], P(('sp', 'ch')), may hold values from -12 to 12
- prompt_ids: int32 [512], P('grp'), parts along dimension 0, may hold values from 0 to 32767
- noise_step: int32 [2], P('grp'), parts along dimension 0, may hold values from 0 to 999
Outputs:
- denoised: bfloat16 [262144, 1024], P(('grp', 'sp', 'ch')), parts along dimension 0
There are 2 independent parts, one for each index of `grp`. A program takes and returns all parts, laid end to end along the dimension named above; an argument that names none is the same for every part. Nothing has to cross between parts.
All inputs are finite; a program needn't handle non-finite values.
Results may differ from a plain program's by a relative error of at most 0.013.
Values may be sent and summed in bfloat16 or wider, within the bound.
A program may use at most 64 MiB of HBM per device.

v0:
```python
import math

import jax
import jax.numpy as jnp
from jax import lax
from jax.sharding import Mesh
from jax.sharding import PartitionSpec as P

TT = 16
HH = 64
WW = 128
C = 1024
SP = ("sp_0", "sp_1")
SP_CH = ("sp_0", "sp_1", "ch")
GRP_SP = ("grp", "sp_0", "sp_1")
GRP_SP_CH = ("grp", "sp_0", "sp_1", "ch")


def in_one_piece(arrays, axis, dim, along):
    ends, at = ([], 0)
    for a in arrays[:-1]:
        at += a.shape[along]
        ends.append(at)
    both = jnp.concatenate(arrays, axis=along)
    return tuple(jnp.split(lax.all_gather(both, axis, axis=dim, tiled=True), ends, axis=along))


def joined_along(parts, dim):
    lengths = list(parts.shape[1:])
    lengths[dim] *= parts.shape[0]
    return jnp.moveaxis(parts, 0, dim).reshape(lengths)


def gather_in_order(value, axes, sequence):
    parts = value[None]
    for k in sequence:
        parts = lax.all_gather(parts, axes[k], axis=0, tiled=True)
    held = [lax.axis_size(axes[k]) for k in reversed(sequence)]
    parts = parts.reshape(*held, *value.shape)
    turned = sorted(range(len(sequence)), key=lambda place: sequence[len(sequence) - 1 - place])
    return parts.transpose(*turned, *range(len(sequence), parts.ndim)).reshape(-1, *value.shape)


def gather_axes(value, axes, sequence, dim):
    return joined_along(gather_in_order(value, axes, sequence), dim)


def cas_table(length):
    position = jnp.arange(length, dtype=jnp.int32)
    product = position[:, None] * position[None, :] % length
    phase_angle = product.astype(jnp.float32) * (2.0 * math.pi / length)
    return ((jnp.cos(phase_angle) + jnp.sin(phase_angle)) / math.sqrt(length)).astype(jnp.bfloat16)


def step_embedding(noise_step, channel, channels):
    half_count = channels // 2
    lower_half = channel < half_count
    position = jnp.where(lower_half, channel, channel - half_count).astype(jnp.float32)
    frequency = jnp.exp(-math.log(10000.0) * position / half_count)
    phase_angle = noise_step[0].astype(jnp.float32) * frequency
    return jnp.where(lower_half, jnp.sin(phase_angle), jnp.cos(phase_angle))


def apply_table(form, table, operand):
    return jnp.einsum(form, table, operand, preferred_element_type=jnp.float32)


def local(latents, spectrum, w_value, w_gate, w_out, embed_table, prompt_ids, noise_step):
    row_count = latents.shape[0]
    chan_part = w_value.shape[1]
    full_value, full_gate, full_out = in_one_piece((w_value, w_gate, w_out), SP, 0, 1)
    value_rows = jnp.dot(latents, full_value, preferred_element_type=jnp.float32).astype(
        jnp.bfloat16
    )
    gate_rows = jnp.dot(latents, full_gate, preferred_element_type=jnp.float32)
    cas_width = cas_table(WW)
    cas_height = cas_table(HH)
    cas_time = cas_table(TT)
    line_grid = value_rows.reshape(row_count // WW, WW, chan_part)
    width_spec = apply_table("kw,lwc->lkc", cas_width, line_grid).astype(jnp.bfloat16)
    pencil = lax.all_to_all(width_spec, SP, split_axis=1, concat_axis=0, tiled=True)
    band_count = pencil.shape[1]
    pencil = pencil.reshape(TT, HH, band_count, chan_part)
    height_spec = apply_table("ah,thkc->takc", cas_height, pencil).astype(jnp.bfloat16)
    full_spec = apply_table("st,takc->sakc", cas_time, height_spec).astype(jnp.bfloat16)
    filtered = (full_spec.astype(jnp.float32) * spectrum.astype(jnp.float32)).astype(jnp.bfloat16)
    time_back = apply_table("ts,sakc->takc", cas_time, filtered).astype(jnp.bfloat16)
    height_back = apply_table("ha,takc->thkc", cas_height, time_back).astype(jnp.bfloat16)
    returned = lax.all_to_all(
        height_back.reshape(TT * HH, band_count, chan_part),
        SP,
        split_axis=0,
        concat_axis=1,
        tiled=True,
    )
    mix_rows = apply_table("wk,lkc->lwc", cas_width, returned).reshape(row_count, chan_part)
    offset = lax.axis_index("ch") * chan_part
    local_pool = jnp.mean(jnp.take(embed_table, prompt_ids, axis=1).astype(jnp.float32), axis=1)
    pooled_all = gather_axes(local_pool, SP_CH, (0, 1, 2), 0)
    pooled = lax.dynamic_slice_in_dim(pooled_all, offset, chan_part)
    channel = offset + jnp.arange(chan_part, dtype=jnp.int32)
    modulation = 1.0 + pooled + step_embedding(noise_step, channel, C)
    mixed_rows = (mix_rows * jax.nn.silu(gate_rows) * modulation[None, :]).astype(jnp.bfloat16)
    half_rows = row_count // lax.axis_size("ch")
    moved_rows = lax.all_to_all(mixed_rows, "ch", split_axis=0, concat_axis=1, tiled=True)
    summed = jnp.dot(moved_rows, full_out, preferred_element_type=jnp.float32)
    residual = lax.dynamic_slice_in_dim(latents, lax.axis_index("ch") * half_rows, half_rows, 0)
    return (residual.astype(jnp.float32) + summed).astype(jnp.bfloat16)


def solution(mesh):
    torus = Mesh(
        mesh.devices.reshape(mesh.shape["grp"], 4, 32, mesh.shape["ch"]),
        ("grp", "sp_0", "sp_1", "ch"),
    )
    in_specs = (
        P(GRP_SP, None),
        P(None, None, SP, "ch"),
        P(SP, "ch"),
        P(SP, "ch"),
        P(SP, None),
        P(SP_CH, None),
        P("grp"),
        P("grp"),
    )
    out_specs = P(GRP_SP_CH, None)
    return jax.shard_map(local, mesh=torus, in_specs=in_specs, out_specs=out_specs, check_vma=False)
```

profile of v0, /device:TPU:33, one launch (start us, length us, event | category | flops | bytes accessed | tf_op | source)
XLA Modules:
  0.0 581.6 jit_solution(15386378072836665653)
XLA Ops:
  6.6 1.3 pad_maximum_fusion
  8.0 278.3 %all-gather.4.cloned.1.call-done = bf16[1024,2048]{1,0:T(8,128)(2,1)} async-done(((bf16[8,2048]{1,0:T(8,128)(2,1)}), bf16[1024,2048]{1,0:T(8,128)(2,1)}) %all-gather.4.cloned.1.call-update) | async-done | bytes 4194320 | tf_op jit(solution)/shard_map/all_gather | solution.py:25
  286.3 3.2 fusion.11
  289.5 0.7 fusion.12
  290.2 0.9 copy.34
  291.1 102.3 %all_to_all.52 = bf16[8,128,512]{2,0,1:T(8,128)(2,1)S(1)} all-to-all(bf16[8,128,512]{2,0,1:T(8,128)(2,1)S(1)} %copy.34), channel_id=1, replica_groups=mesh['grp'=2,'sp_0'=4,'sp_1'=32,'ch'=2] {'sp_0','sp_1'}, dimensions={1} | all-to-all | bytes 2097152 | tf_op jit(solution)/shard_map/all_to_all | solution.py:81
  393.9 1.6 convolution_convert_fusion.2
  395.5 1.5 convolution_convert_fusion
  397.6 1.5 reduce.1
  399.0 1.2 reshape.84
  400.2 17.1 %all-to-all-start.1 = ((bf16[128,2,2048]{2,1,0:T(2,128)(2,1)}), bf16[128,2,2048]{2,1,0:T(2,128)(2,1)S(1)}, u32[]{:S(2)}, u32[]{:S(2)}) async-start(bf16[128,2,2048]{2,1,0:T(2,128)(2,1)} %reshape.84), calls=%async_computation.1 | async-start | bytes 2097152 | tf_op jit(solution)/shard_map/all_to_all | solution.py:89
  417.4 5.7 copy.41
  423.1 1.3 dynamic-slice
  425.1 5.2 gather_fusion
  430.6 7.9 %all-reduce = f32[16]{0:T(128)S(1)} all-reduce(f32[16]{0:T(128)S(1)} %multiply_dynamic-update-slice_fusion), channel_id=2, replica_groups=mesh['grp'=2,'sp_0'=4,'sp_1'=32,'ch'=2] {'sp_0'}, use_global_device_ids=true, to_apply=%add | all-reduce | flops 16 | bytes 128
  438.6 92.9 %all-gather.1 = f32[32,4,4]{2,1,0:T(4,128)S(1)} all-gather(f32[1,4,4]{2,1,0:T(4,128)S(1)} %reshape.76), channel_id=1, replica_groups=mesh['grp'=2,'sp_0'=4,'sp_1'=32,'ch'=2] {'sp_1'}, dimensions={0}, use_global_device_ids=true | all-gather | bytes 2112 | tf_op jit(solution)/shard_map/all_gather | solution.py:37
  531.6 25.7 %all_gather.15 = f32[256,4]{0,1:T(4,128)S(1)} all-gather(f32[128,4]{0,1:T(4,128)S(1)} %copy.42), channel_id=1, replica_groups=mesh['grp'=2,'sp_0'=4,'sp_1'=32,'ch'=2] {'ch'}, dimensions={0}, use_global_device_ids=true | all-gather | bytes 6144 | tf_op jit(solution)/shard_map/all_gather | solution.py:37
  557.4 0.6 copy.43
  558.9 1.1 reshape.85
  560.3 1.1 fusion.20
  561.4 1.9 copy.40
  563.2 4.3 fusion.8
  567.7 4.8 all_to_all.53
  572.5 2.2 add_convert_fusion
  (28 shorter events, 2.3 us)
Async XLA Ops:
  6.5 279.7 %all-gather.4.cloned.1.call-start = ((), (), s32[]{:S(2)}) async-start(), calls=%async_computation.3 | async-start | bytes 4227072 | tf_op jit(solution)/shard_map/all_gather | solution.py:25
  291.1 102.8 %copy-start = (bf16[16,64,1,512]{3,1,2,0:T(8,128)(2,1)S(1)}, bf16[16,64,1,512]{3,1,2,0:T(8,128)(2,1)}, u32[]{:S(2)}) copy-start(bf16[16,64,1,512]{3,1,2,0:T(8,128)(2,1)} %param.9) | copy-start | bytes 3145732
  399.0 18.4 %copy-start.1 = (bf16[4,32768]{1,0:T(4,128)(2,1)S(1)}, bf16[4,32768]{1,0:T(4,128)(2,1)}, u32[]{:S(2)}) copy-start(bf16[4,32768]{1,0:T(4,128)(2,1)} %param.13) | copy-start | bytes 786436
  400.2 158.7 %all-to-all-start.1 = ((bf16[128,2,2048]{2,1,0:T(2,128)(2,1)}), bf16[128,2,2048]{2,1,0:T(2,128)(2,1)S(1)}, u32[]{:S(2)}, u32[]{:S(2)}) async-start(bf16[128,2,2048]{2,1,0:T(2,128)(2,1)} %reshape.84), calls=%async_computation.1 | async-start | bytes 2097152 | tf_op jit(solution)/shard_map/all_to_all | solution.py:89
  417.4 7.7 %copy-start.2 = (s32[256]{0:T(256)S(1)}, s32[256]{0:T(256)}, u32[]{:S(2)}) copy-start(s32[256]{0:T(256)} %param.14) | copy-start | bytes 3076
  563.2 9.3 %copy-start.4 = (bf16[1024,1024]{1,0:T(8,128)(2,1)S(1)}, bf16[1024,1024]{1,0:T(8,128)(2,1)}, u32[]{:S(2)}) copy-start(bf16[1024,1024]{1,0:T(8,128)(2,1)} %param.8) | copy-start | bytes 6291460
  567.6 4.9 copy-start.3
Sparse Core Ops, SparseCore 0:
  10.3 275.8 all-gather.3
where the time goes:
time: 583 us; the launch traced here: 582 us
  waiting for transfers between devices  278 us (48%)
  blocking collectives  234 us (40%)
  local copies, waits for them, and re-layouts  19.3 us (3%)
  starting transfers between devices  17.1 us (3%)
  matrix products  15.2 us (3%)
  between operations  14.9 us (3%)
    all_gather x1, waiting for transfers between devices, in_one_piece(): lax.all_gather(both, axis, axis=dim, tiled=True)  278 us
    all_gather x2, blocking collectives, gather_in_order(): parts = lax.all_gather(parts, axes[k], axis=0, tiled=True)  119 us
    all_to_all x1, blocking collectives, local(): lax.all_to_all(width_spec, SP, split_axis=1, concat_axis=0, tiled=True)  102 us
    all_to_all x1, starting transfers between devices, local(): lax.all_to_all(height_back.reshape(TT * HH, band_count, chan_part), SP, s...  17.1 us
  transfers between devices with their start and end apart: 2, of which 1 were waited for; matrix products, arithmetic and copies ran while one was open for 2% of the time, Pallas kernels for 0%

commit v1 on v0

v1 whole, which is shorter than its diff:
```python
import math

import jax
import jax.numpy as jnp
from jax import lax
from jax.sharding import Mesh
from jax.sharding import PartitionSpec as P

TT = 16
HH = 64
WW = 128
C = 1024
SP = ("sp_0", "sp_1")
SP_CH = ("sp_0", "sp_1", "ch")
GRP_SP = ("grp", "sp_0", "sp_1")
GRP_SP_CH = ("grp", "sp_0", "sp_1", "ch")
F32 = jnp.float32
BF16 = jnp.bfloat16


def cas_table(length):
    position = jnp.arange(length, dtype=jnp.int32)
    product = position[:, None] * position[None, :] % length
    phase_angle = product.astype(jnp.float32) * (2.0 * math.pi / length)
    return ((jnp.cos(phase_angle) + jnp.sin(phase_angle)) / math.sqrt(length)).astype(jnp.bfloat16)


def step_embedding(noise_step, channel, channels):
    half_count = channels // 2
    lower_half = channel < half_count
    position = jnp.where(lower_half, channel, channel - half_count).astype(jnp.float32)
    frequency = jnp.exp(-math.log(10000.0) * position / half_count)
    phase_angle = noise_step[0].astype(jnp.float32) * frequency
    return jnp.where(lower_half, jnp.sin(phase_angle), jnp.cos(phase_angle))


def dot(a, b):
    return jnp.dot(a, b, preferred_element_type=F32)


def local_pool(embed_table, prompt_ids):
    vocab = embed_table.shape[1]
    low = 256
    high_hot = (prompt_ids[:, None] // low == jnp.arange(vocab // low)[None, :]).astype(BF16)
    low_hot = (prompt_ids[:, None] % low == jnp.arange(low)[None, :]).astype(BF16)
    counts = jnp.einsum("ph,pl->hl", high_hot, low_hot, preferred_element_type=F32)
    total = jnp.sum(embed_table.astype(F32) * counts.reshape(1, vocab), axis=1)
    return total / prompt_ids.shape[0]


def local(latents, spectrum, w_value, w_gate, w_out, embed_table, prompt_ids, noise_step):
    row_count = latents.shape[0]
    part = w_value.shape[1]
    lines = row_count // WW
    core = lax.axis_index("ch")
    offset = core * part

    pool4 = local_pool(embed_table, prompt_ids)
    pool8 = lax.all_gather(pool4, "ch", axis=0, tiled=True)
    high = lax.reduce_precision(pool8, 8, 7)
    low = pool8 - high
    pool_cols = jnp.pad(jnp.stack([high, low], axis=1), ((0, 0), (0, 126))).astype(BF16)
    packed = jnp.concatenate([w_value, w_gate, w_out, pool_cols], axis=1)
    column = lax.all_gather(packed, "sp_1", axis=0, tiled=True)
    weights = lax.all_gather(column, "sp_0", axis=0, tiled=True)

    cas_width = cas_table(WW)
    space = jnp.einsum("st,ah->sath", cas_table(TT).astype(F32), cas_table(HH).astype(F32))
    space = space.reshape(TT * HH, TT * HH).astype(BF16)

    mine = lax.dynamic_slice_in_dim(latents, offset, part, 1).reshape(lines, WW, part)
    spread = jnp.einsum("kw,lwc->klc", cas_width, mine, preferred_element_type=F32).astype(BF16)
    arrived = lax.all_to_all(spread, SP, split_axis=0, concat_axis=0, tiled=True)
    arrived = arrived.reshape(TT * HH, part)
    both = lax.all_gather(arrived, "ch", axis=1, tiled=True)
    width_spec = dot(both, weights[:, :part]).astype(BF16)
    full_spec = dot(space, width_spec).astype(BF16)
    gains = spectrum.reshape(TT * HH, part)
    filtered = (full_spec.astype(F32) * gains.astype(F32)).astype(BF16)
    height_back = dot(space, filtered).astype(BF16)
    returned = lax.all_to_all(
        height_back.reshape(-1, lines, part), SP, split_axis=0, concat_axis=0, tiled=True
    )
    gate_rows = dot(latents, weights[:, part : 2 * part])
    pooled_all = weights[:, 2 * part + C].astype(F32) + weights[:, 2 * part + C + 1].astype(F32)
    pooled = lax.dynamic_slice_in_dim(pooled_all, offset, part)
    channel = offset + jnp.arange(part, dtype=jnp.int32)
    modulation = 1.0 + pooled + step_embedding(noise_step, channel, C)
    gain = jax.nn.silu(gate_rows) * modulation[None, :]
    mix_rows = jnp.einsum("wk,klc->lwc", cas_width, returned, preferred_element_type=F32)
    mixed = (mix_rows.reshape(row_count, part) * gain).astype(BF16)
    half = row_count // lax.axis_size("ch")
    moved = lax.all_to_all(mixed, "ch", split_axis=0, concat_axis=1, tiled=True)
    summed = dot(moved, weights[:, 2 * part : 2 * part + C])
    residual = lax.dynamic_slice_in_dim(latents, core * half, half, 0)
    return (residual.astype(F32) + summed).astype(BF16)


def solution(mesh):
    torus = Mesh(
        mesh.devices.reshape(mesh.shape["grp"], 4, 32, mesh.shape["ch"]),
        ("grp", "sp_0", "sp_1", "ch"),
    )
    in_specs = (
        P(GRP_SP, None),
        P(None, None, SP, "ch"),
        P(SP, "ch"),
        P(SP, "ch"),
        P(SP, None),
        P(SP_CH, None),
        P("grp"),
        P("grp"),
    )
    out_specs = P(GRP_SP_CH, None)
    return jax.shard_map(local, mesh=torus, in_specs=in_specs, out_specs=out_specs, check_vma=False)
```

time: 583 us -> 465 us (0.80)
  blocking collectives: 234 us -> 50.3 us
  waiting for transfers between devices: 278 us -> 319 us
  starting transfers between devices: 17.1 us -> 41.1 us
    all_gather x2 -> x0, blocking collectives: 119 us -> none  [gather_in_order(): parts = lax.all_gather(parts, axes[k], axis=0, tiled=True)]
    all_to_all x1 -> x2, waiting for transfers between devices: 0.01 us -> 102 us  [the longest x1 102 us: local(): lax.all_to_all(height_back.reshape(-1, lines, part), SP, split_axis=0, co...]
    all_to_all x2 -> x1, blocking collectives: 107 us -> 6.7 us  [local(): moved = lax.all_to_all(mixed, 'ch', split_axis=0, concat_axis=1, tiled=True)]
    all_gather x1 -> x3, waiting for transfers between devices: 278 us -> 217 us  [the longest x1 119 us: local(): column = lax.all_gather(packed, 'sp_1', axis=0, tiled=True)]
    unnamed x1, blocking collectives: 7.93 us -> 43.6 us
    all_to_all x1 -> x2, starting transfers between devices: 17.1 us -> 41 us  [the longest x1 28.1 us: local(): lax.all_to_all(height_back.reshape(-1, lines, part), SP, split_axis=0, co...]
    unnamed x18 -> x10, local copies, waits for them, and re-layouts: 9.79 us -> 2.41 us
    convert_element_type x1 -> x2, local copies, waits for them, and re-layouts: 0.9 us -> 7.11 us  [the longest x1 5.56 us: local(): space = space.reshape(TT * HH, TT * HH).astype(BF16)]
  transfers between devices with their start and end apart: 2 -> 5, of which waited for: 1 -> 4; matrix products, arithmetic and copies ran while one was open for 2% -> 3% of each run, Pallas kernels for 0% -> 0%
where the time goes in v1:
time: 465 us; the launch traced here: 464 us
  waiting for transfers between devices  319 us (69%)
  blocking collectives  50.3 us (11%)
  starting transfers between devices  41.1 us (9%)
  matrix products  18.7 us (4%)
  between operations  14.6 us (3%)
  local copies, waits for them, and re-layouts  13.9 us (3%)
  other arithmetic  6.88 us (1%)
    all_gather x1, waiting for transfers between devices, local(): column = lax.all_gather(packed, 'sp_1', axis=0, tiled=True)  119 us
    all_to_all x1, waiting for transfers between devices, local(): lax.all_to_all(height_back.reshape(-1, lines, part), SP, split_axis=0, co...  102 us
    all_gather x1, waiting for transfers between devices, local(): weights = lax.all_gather(column, 'sp_0', axis=0, tiled=True)  62.7 us
    unnamed x1, blocking collectives  43.6 us
    all_gather x1, waiting for transfers between devices, local(): both = lax.all_gather(arrived, 'ch', axis=1, tiled=True)  35.1 us
    all_to_all x1, starting transfers between devices, local(): lax.all_to_all(height_back.reshape(-1, lines, part), SP, split_axis=0, co...  28.1 us
    dot_general x4, matrix products, dot(): return jnp.dot(a, b, preferred_element_type=F32)  16.7 us
    all_to_all x1, starting transfers between devices, local(): lax.all_to_all(spread, SP, split_axis=0, concat_axis=0, tiled=True)  12.9 us
  transfers between devices with their start and end apart: 5, of which 4 were waited for; matrix products, arithmetic and copies ran while one was open for 3% of the time, Pallas kernels for 0%

profile of v1, /device:TPU:33, one launch (start us, length us, event | category | flops | bytes accessed | tf_op | source)
XLA Modules:
  0.0 464.0 jit_solution(6335007486320289089)
XLA Ops:
  6.6 0.7 and_select_fusion.1
  7.6 1.3 dynamic-slice.1
  9.5 1.3 multiply_reduce_fusion
  11.0 43.6 %all-reduce.1 = f32[8]{0:T(128)S(1)} all-reduce(f32[8]{0:T(128)S(1)} %multiply_dynamic-update-slice_fusion), channel_id=1, replica_groups=mesh['grp'=2,'sp_0'=4,'sp_1'=32,'ch'=2] {'ch'}, use_global_device_ids=true, to_apply=%add.1 | all-reduce | flops 8 | bytes 64
  54.7 1.4 fusion.28
  56.1 1.3 constant_dynamic-slice_fusion
  58.1 1.5 copy.17
  59.6 12.9 %all-to-all-start = ((bf16[128,8,512]{2,1,0:T(8,128)(2,1)}), bf16[128,8,512]{2,1,0:T(8,128)(2,1)S(1)}, u32[]{:S(2)}, u32[]{:S(2)}) async-start(bf16[128,8,512]{2,1,0:T(8,128)(2,1)} %copy.17), calls=%async_computation | async-start | bytes 2097152 | tf_op jit(solution)/shard_map/all_to_all | solution.py:73
  72.6 118.9 %all-gather.6.cloned.1.call-done = bf16[256,2176]{1,0:T(8,128)(2,1)} async-done(((bf16[8,2176]{1,0:T(8,128)(2,1)}), bf16[256,2176]{1,0:T(8,128)(2,1)}) %all-gather.6.cloned.1.call-update) | async-done | bytes 1114128 | tf_op jit(solution)/shard_map/all_gather | solution.py:64
  191.7 1.0 copy-done
  192.9 3.0 fusion
  195.9 5.6 %convert_element_type.98 = bf16[1024,1024]{1,0:T(8,128)(2,1)S(1)} reshape(bf16[16,64,16,64]{3,2,1,0:T(8,128)(2,1)} %fusion) | data formatting | bytes 4194304 | tf_op jit(solution)/shard_map/convert_element_type | solution.py:69
  201.4 62.7 %all-gather.8.cloned.1.call-done = bf16[1024,2176]{1,0:T(8,128)(2,1)} async-done(((bf16[256,2176]{1,0:T(8,128)(2,1)}), bf16[1024,2176]{1,0:T(8,128)(2,1)}) %all-gather.8.cloned.1.call-update) | async-done | bytes 4456464 | tf_op jit(solution)/shard_map/all_gather | solution.py:65
  264.2 35.1 %all-gather.4.cloned.1.call-done = bf16[1024,1024]{1,0:T(8,128)(2,1)} async-done(((bf16[1024,512]{1,0:T(8,128)(2,1)}), bf16[1024,1024]{1,0:T(8,128)(2,1)}) %all-gather.4.cloned.1.call-update) | async-done | bytes 2097168 | tf_op jit(solution)/shard_map/all_gather | solution.py:75
  299.3 5.2 %fusion.3 = bf16[1024,512]{1,0:T(8,128)(2,1)} fusion(bf16[1024,512]{1,0:T(8,128)(2,1)S(1)} %bitcast.64, bf16[1024,1024]{1,0:T(8,128)(2,1)S(1)} %convert_element_type.98, bf16[1024,1024]{1,0:T(8,128)(2,1)} %all-gather.4.cloned.1.call-done, bf16[1024,2176]{1,0:T(8,128)(2,1)} %all-gather.8.cloned.1.call-done), kind=kOutput, calls=%fused_computation.5 | convolution fusion | flops 2150629376 | bytes 7340032 | tf_op jit(solution)/shard_map/dot_general | solution.py:38
  304.5 3.5 fusion.12
  307.9 28.1 %all-to-all-start.1 = ((bf16[128,8,512]{2,1,0:T(8,128)(2,1)}), bf16[128,8,512]{2,1,0:T(8,128)(2,1)S(1)}, u32[]{:S(2)}, u32[]{:S(2)}) async-start(bf16[128,8,512]{2,1,0:T(8,128)(2,1)} %fusion.12), calls=%async_computation.1 | async-start | bytes 2097152 | tf_op jit(solution)/shard_map/all_to_all | solution.py:81
  336.7 1.2 fusion.70
  338.1 101.6 %all-to-all-done.1 = bf16[128,8,512]{2,1,0:T(8,128)(2,1)S(1)} async-done(((bf16[128,8,512]{2,1,0:T(8,128)(2,1)}), bf16[128,8,512]{2,1,0:T(8,128)(2,1)S(1)}, u32[]{:S(2)}, u32[]{:S(2)}) %all-to-all-start.1) | async-done | bytes 1048608 | tf_op jit(solution)/shard_map/all_to_all | solution.py:81
  439.7 1.1 fusion.15
  440.8 1.9 copy.20
  442.6 4.2 fusion.9
  446.9 6.7 %all_to_all.29 = bf16[2,512,512]{1,2,0:T(8,128)(2,1)S(1)} all-to-all(bf16[2,512,512]{1,2,0:T(8,128)(2,1)S(1)} %bitcast.60), channel_id=1, replica_groups=mesh['grp'=2,'sp_0'=4,'sp_1'=32,'ch'=2] {'ch'}, dimensions={0} | all-to-all | bytes 2097152 | tf_op jit(solution)/shard_map/all_to_all | solution.py:93
  453.6 3.8 add_convert_fusion
  (25 shorter events, 2.0 us)
Async XLA Ops:
  6.5 185.0 %all-gather.6.cloned.1.call-start = ((), (), s32[]{:S(2)}) async-start(), calls=%async_computation.4 | async-start | bytes 1148928 | tf_op jit(solution)/shard_map/all_gather | solution.py:64
  59.6 132.0 %all-to-all-start = ((bf16[128,8,512]{2,1,0:T(8,128)(2,1)}), bf16[128,8,512]{2,1,0:T(8,128)(2,1)S(1)}, u32[]{:S(2)}, u32[]{:S(2)}) async-start(bf16[128,8,512]{2,1,0:T(8,128)(2,1)} %copy.17), calls=%async_computation | async-start | bytes 2097152 | tf_op jit(solution)/shard_map/all_to_all | solution.py:73
  72.5 191.7 %all-gather.8.cloned.1.call-start = ((), (), s32[]{:S(2)}) async-start(), calls=%async_computation.5 | async-start | bytes 5570560 | tf_op jit(solution)/shard_map/all_gather | solution.py:65
  191.6 107.7 %all-gather.4.cloned.1.call-start = ((), (), s32[]{:S(2)}) async-start(), calls=%async_computation.3 | async-start | bytes 3145728 | tf_op jit(solution)/shard_map/all_gather | solution.py:75
  191.7 1.0 copy-start
  195.9 103.4 %copy-start.2 = (bf16[16,64,1,512]{3,1,2,0:T(8,128)(2,1)S(1)}, bf16[16,64,1,512]{3,1,2,0:T(8,128)(2,1)}, u32[]{:S(2)}) copy-start(bf16[16,64,1,512]{3,1,2,0:T(8,128)(2,1)} %param.9) | copy-start | bytes 3145732
  307.9 131.8 %all-to-all-start.1 = ((bf16[128,8,512]{2,1,0:T(8,128)(2,1)}), bf16[128,8,512]{2,1,0:T(8,128)(2,1)S(1)}, u32[]{:S(2)}, u32[]{:S(2)}) async-start(bf16[128,8,512]{2,1,0:T(8,128)(2,1)} %fusion.12), calls=%async_computation.1 | async-start | bytes 2097152 | tf_op jit(solution)/shard_map/all_to_all | solution.py:81
  446.8 6.8 %copy-start.1 = (bf16[1024,1024]{1,0:T(8,128)(2,1)S(1)}, bf16[1024,1024]{1,0:T(8,128)(2,1)}, u32[]{:S(2)}) copy-start(bf16[1024,1024]{1,0:T(8,128)(2,1)} %param.8) | copy-start | bytes 6291460
Sparse Core Ops, SparseCore 0:
  56.2 135.2 all-gather.5
  193.6 70.4 all-gather.7
  266.3 32.9 all-gather.3

commit v2 on v1

v2 whole, which is shorter than its diff:
```python
import functools
import math

import jax
import jax.numpy as jnp
import numpy as np
from jax import lax
from jax.experimental import pallas as pl
from jax.experimental.pallas import tpu as pltpu
from jax.sharding import Mesh
from jax.sharding import PartitionSpec as P

TT = 16
HH = 64
WW = 128
SP_CH = ("sp_0", "sp_1", "ch")
GRP_SP = ("grp", "sp_0", "sp_1")
GRP_SP_CH = ("grp", "sp_0", "sp_1", "ch")
SP = ("sp_0", "sp_1")
F32 = jnp.float32
BF16 = jnp.bfloat16
MESH = pl.DeviceIdType.MESH
STRIDE = 4
WINDOW = 16


def cas_table(length):
    position = np.arange(length, dtype=np.int32)
    product = position[:, None] * position[None, :] % length
    phase_angle = product.astype(np.float32) * np.float32(2.0 * math.pi / length)
    table = (np.cos(phase_angle) + np.sin(phase_angle)) / np.float32(math.sqrt(length))
    return jnp.asarray(table.astype(jnp.bfloat16))


def step_embedding(noise_step, channel, channels):
    half_count = channels // 2
    lower_half = channel < half_count
    position = jnp.where(lower_half, channel, channel - half_count).astype(jnp.float32)
    frequency = jnp.exp(-math.log(10000.0) * position / half_count)
    phase_angle = noise_step[0].astype(jnp.float32) * frequency
    return jnp.where(lower_half, jnp.sin(phase_angle), jnp.cos(phase_angle))


def dot(a, b):
    return jnp.dot(a, b, preferred_element_type=F32)


def iota(shape, dim):
    return lax.broadcasted_iota(jnp.int32, shape, dim)


def one_hot(condition):
    return jnp.where(condition, 1.0, 0.0).astype(BF16)


def kernel(
    nx, nz,
    lat, spec, wv_in, wg_in, wo_in, table, ids, emb, kw, kh, kt,
    out,
    spread, arrived, spin, spout, back, returned, y_own, y_other, filt, gain,
    wv, wgo, wo_other, mix_own, mix_other, counts, space, wide, narrow,
    a_send, a_recv, b_send, b_recv, s_send, s_recv, r_send, r_recv, x_send, x_recv,
    y_send, y_recv, o_send, o_recv, m_send, m_recv,
):
    n = nx * nz
    rows, chans = lat.shape
    part = wv_in.shape[1]
    lines = rows // WW
    block = rows // n
    mx, mz, core = lax.axis_index("sp_0"), lax.axis_index("sp_1"), lax.axis_index("ch")
    me = mx * nz + mz
    other_core = {"ch": 1 - core}

    def partner(i):
        j = n - 1 - i
        zi, dx = j // nx, j % nx
        m = (zi + 1) // 2
        dz = jnp.where(zi % 2 == 1, m, nz - m) % nz
        tx, tz = (mx + dx) % nx, (mz + dz) % nz
        return {"sp_0": tx, "sp_1": tz}, tx * nz + tz

    barrier = pltpu.get_barrier_semaphore()

    def greet(i, carry):
        device, _ = partner(i)
        pl.semaphore_signal(barrier, inc=1, device_id=device, device_id_type=MESH)
        return carry

    lax.fori_loop(0, n - 1, greet, 0)
    pl.semaphore_signal(barrier, inc=1, device_id=other_core, device_id_type=MESH)

    pick = one_hot(iota((rows, WW), 0) // lines == iota((rows, WW), 1))
    spread_rows = dot(pick, kw[...]).astype(BF16)
    line_of = iota((rows, WW), 0) % lines
    for line in range(lines):
        narrow[:, line * WW : (line + 1) * WW] = jnp.where(
            line_of == line, spread_rows, jnp.zeros_like(spread_rows)
        )
    mine = pl.ds(pl.multiple_of(core * part, 128), part)
    tile = 256
    per = tile // block

    def widen(r, carry):
        at = pl.ds(pl.multiple_of(r * tile, tile), tile)
        got = dot(narrow[at, :], lat[:, mine]).astype(BF16)
        spread[pl.ds(r * per, per)] = got.reshape(per, block, part)
        return carry

    lax.fori_loop(0, rows // tile, widen, 0)
    arrived[me] = spread[me]
    wv[mx, mz // STRIDE, mz % STRIDE] = wv_in[...]
    wgo[mx, mz // STRIDE, mz % STRIDE, :, 0:part] = wg_in[...]
    wgo[mx, mz // STRIDE, mz % STRIDE, :, part : 2 * part] = wo_in[:, mine]

    pl.semaphore_wait(barrier, n)

    groups = nz // STRIDE
    up = (groups + 1) // 2
    down = groups - 1 - up

    def hop(stream, direction, q):
        buf = (wv, wgo)[stream]
        origin = (mz // STRIDE - direction * (q - 1) + groups) % groups
        ref = buf.at[mx, origin, mz % STRIDE]
        k = (q - 1) if direction > 0 else up + q - 1
        return pltpu.make_async_remote_copy(
            src_ref=ref, dst_ref=ref,
            send_sem=s_send.at[stream, k], recv_sem=s_recv.at[stream, k],
            device_id={"sp_1": (mz + direction * STRIDE + nz) % nz}, device_id_type=MESH,
        )

    def near(stream, k):
        buf = (wv, wgo)[stream]
        ref = buf.at[mx, :, mz % STRIDE]
        step = (1, -1, 2)[k]
        return pltpu.make_async_remote_copy(
            src_ref=ref, dst_ref=ref,
            send_sem=r_send.at[stream, k], recv_sem=r_recv.at[stream, k],
            device_id={"sp_1": (mz + step + nz) % nz}, device_id_type=MESH,
        )

    def across(stream, k):
        buf = (wv, wgo)[stream]
        ref = buf.at[mx]
        return pltpu.make_async_remote_copy(
            src_ref=ref, dst_ref=ref,
            send_sem=x_send.at[stream, k], recv_sem=x_recv.at[stream, k],
            device_id={"sp_0": (mx + k + 1) % nx}, device_id_type=MESH,
        )

    def near_in(stream, k):
        buf = (wv, wgo)[stream]
        step = (1, -1, 2)[k]
        ref = buf.at[mx, :, (mz - step + nz) % STRIDE]
        return pltpu.make_async_copy(ref, ref, r_recv.at[stream, k])

    def gather_step(stream, step):
        if 0 < step <= up:
            hop(stream, 1, step).wait_recv()
        if 0 < step <= down:
            hop(stream, -1, step).wait_recv()
        if step < up:
            hop(stream, 1, step + 1).start()
        if step < down:
            hop(stream, -1, step + 1).start()
        if step == up:
            for k in range(3):
                near(stream, k).start()
        if step == up + 1:
            for k in range(3):
                near_in(stream, k).wait()
            for k in range(nx - 1):
                across(stream, k).start()
        if step == up + 2:
            for k in range(nx - 1):
                across(stream, k).wait_recv()
            for q in range(up):
                hop(stream, 1, q + 1).wait_send()
            for q in range(down):
                hop(stream, -1, q + 1).wait_send()
            for k in range(3):
                near(stream, k).wait_send()
            for k in range(nx - 1):
                across(stream, k).wait_send()

    def exchange(src, dst, send_sem, recv_sem):
        def copy(i):
            device, target = partner(i)
            return pltpu.make_async_remote_copy(
                src_ref=src.at[target], dst_ref=dst.at[me],
                send_sem=send_sem.at[i], recv_sem=recv_sem.at[0],
                device_id=device, device_id_type=MESH,
            )

        def send(first, last):
            def body(i, carry):
                @pl.when(i >= WINDOW)
                def _():
                    copy(i - WINDOW).wait_send()

                copy(i).start()
                return carry

            lax.fori_loop(first, last, body, 0)

        def drain():
            def body(i, carry):
                copy(i).wait_send()
                return carry

            lax.fori_loop(n - 1 - WINDOW, n - 1, body, 0)
            some = dst.at[pl.ds(0, n - 1)]
            pltpu.make_async_copy(some, some, recv_sem.at[0]).wait()

        return send, drain

    send, drain = exchange(spread, arrived, a_send, a_recv)
    gather_step(0, 0)
    send(0, 8)

    vocab = table.shape[1]
    low_count = 256
    high_count = vocab // low_count
    prompt = ids.shape[0]
    high_hot = one_hot(ids[...] // low_count == iota((prompt, high_count), 1))
    low_hot = one_hot(ids[...] % low_count == iota((prompt, low_count), 1))
    counts[...] = lax.dot_general(
        high_hot, low_hot, (((0,), (0,)), ((), ())), preferred_element_type=F32
    )

    def tally(h, total):
        piece = table[:, pl.ds(pl.multiple_of(h * low_count, low_count), low_count)]
        return total + piece.astype(F32) * counts[pl.ds(h, 1), :]

    few = table.shape[0]
    total = lax.fori_loop(0, high_count, tally, jnp.zeros((few, low_count), F32))
    pooled4 = jnp.sum(total, axis=1, keepdims=True) * (1.0 / prompt)
    pooled8 = jnp.concatenate([pooled4] * (block // few), axis=0)
    pooled8 = jnp.where(iota((block, 1), 0) // few == core, pooled8, 0.0)
    first = pooled8.astype(BF16).astype(F32)
    second = (pooled8 - first).astype(BF16).astype(F32)
    third = pooled8 - first - second
    lane = iota((block, 128), 1)
    terms = jnp.where(lane == 0, first, jnp.where(lane == 1, second, jnp.where(lane == 2, third, 0.0)))
    wgo[mx, mz // STRIDE, mz % STRIDE, :, 2 * part : 2 * part + 128] = terms.astype(BF16)

    at = 8
    total_steps = up + 3
    for step in range(1, total_steps):
        send(at, at + 8)
        at += 8
        gather_step(0, step)
    gather_step(1, 0)
    cells = TT * HH
    kt_wide = dot(kt[...], one_hot(iota((TT, cells), 1) // HH == iota((TT, cells), 0)))
    kh_wide = dot(kh[...], one_hot(iota((HH, cells), 1) % HH == iota((HH, cells), 0)))
    for s in range(TT):
        space[s * HH : (s + 1) * HH, :] = (kh_wide * kt_wide[s : s + 1, :]).astype(BF16)
    kw_wide = dot(kw[...], one_hot(iota((WW, rows), 1) // lines == iota((WW, rows), 0)))
    column_line = iota((WW, rows), 1) % lines
    for line in range(lines):
        wide[line * WW : (line + 1) * WW, :] = jnp.where(column_line == line, kw_wide, 0.0).astype(BF16)
    for step in range(1, total_steps):
        send(at, at + 8)
        at += 8
        gather_step(1, step)
    upper = pl.ds(part, part + 128)
    swap_out = pltpu.make_async_remote_copy(
        src_ref=wgo.at[:, :, :, :, upper], dst_ref=wo_other, send_sem=o_send, recv_sem=o_recv,
        device_id=other_core, device_id_type=MESH,
    )
    swap_out.start()
    send(at, n - 1)
    drain()

    quarters = rows // tile
    ycopies = []
    for r in range(quarters):
        here = slice(r * tile, (r + 1) * tile)
        full = arrived[...].reshape(rows, part)
        y_own[here, :] = dot(space[here, :], full).astype(BF16)
        ycopies.append(pltpu.make_async_remote_copy(
            src_ref=y_own.at[pl.ds(r * tile, tile)], dst_ref=y_other.at[pl.ds(r * tile, tile)],
            send_sem=y_send.at[r], recv_sem=y_recv.at[r], device_id=other_core, device_id_type=MESH,
        ))
        ycopies[-1].start()
    weight = wv.reshape(chans, part)
    own_rows = pl.ds(pl.multiple_of(core * part, part), part)
    other_rows = pl.ds(pl.multiple_of((1 - core) * part, part), part)
    for r in range(quarters):
        here = slice(r * tile, (r + 1) * tile)
        ycopies[r].wait_recv()
        value = dot(y_own[here, :], weight[own_rows, :]) + dot(y_other[here, :], weight[other_rows, :])
        filt[here, :] = (value * spec[here, :].astype(F32)).astype(BF16)
    for r in range(quarters):
        here = slice(r * tile, (r + 1) * tile)
        got = dot(space[here, :], filt[...]).astype(BF16)
        back[r * per : (r + 1) * per] = got.reshape(per, block, part)
        ycopies[r].wait_send()
    returned[me] = back[me]
    send, drain = exchange(back, returned, b_send, b_recv)
    send(0, n - 1)

    swap_out.wait()
    gathered = wgo.reshape(chans, 2 * part + 128)
    others = wo_other.reshape(chans, part + 128)
    pools = gathered[:, 2 * part : 2 * part + 128] + others[:, part : part + 128]
    chosen = one_hot(iota((chans, part), 0) == iota((chans, part), 1) + core * part)
    terms = lax.dot_general(pools, chosen, (((0,), (0,)), ((), ())), preferred_element_type=F32)
    modulation = 1.0 + jnp.sum(terms[0:8, :], axis=0, keepdims=True) + emb[...]

    def gate(r, carry):
        here = pl.ds(pl.multiple_of(r * tile, tile), tile)
        v = dot(lat[here, :], gathered[:, 0:part])
        gain[here, :] = v / (1.0 + jnp.exp(-v)) * modulation
        return carry

    lax.fori_loop(0, quarters, gate, 0)
    drain()

    half = rows // 2

    def finish(r, dst, base):
        here = pl.ds(pl.multiple_of(base + r * tile, tile), tile)
        mix = dot(wide[here, :], returned[...].reshape(rows, part)) * gain[here, :]
        dst[pl.ds(pl.multiple_of(r * tile, tile), tile), :] = mix.astype(BF16)

    mcopies = []
    for r in range(half // tile):
        finish(r, spout, (1 - core) * half)
        mcopies.append(pltpu.make_async_remote_copy(
            src_ref=spout.at[pl.ds(r * tile, tile)], dst_ref=mix_other.at[pl.ds(r * tile, tile)],
            send_sem=m_send.at[r], recv_sem=m_recv.at[r], device_id=other_core, device_id_type=MESH,
        ))
        mcopies[-1].start()
    for r in range(half // tile):
        finish(r, mix_own, core * half)
    left = pl.ds(pl.multiple_of(core * part, part), part)
    right = pl.ds(pl.multiple_of((1 - core) * part, part), part)
    for r in range(half // tile):
        here = slice(r * tile, (r + 1) * tile)
        mcopies[r].wait()
        for at, weight in ((left, gathered.at[:, part : 2 * part]), (right, others.at[:, 0:part])):
            out[here, at] = dot(mix_own[here, :], weight[own_rows, :]) + dot(
                mix_other[here, :], weight[other_rows, :]
            )


def local(nx, nz, latents, spectrum, w_value, w_gate, w_out, embed_table, prompt_ids, noise_step):
    rows, chans = latents.shape
    block, part = w_value.shape
    n = nx * nz
    core = lax.axis_index("ch")
    channel = core * part + jnp.arange(part, dtype=jnp.int32)
    emb = step_embedding(noise_step, channel, chans).reshape(1, part)
    half = rows // 2
    groups = nz // STRIDE
    hops = groups - 1
    vmem = pl.BlockSpec(memory_space=pltpu.VMEM)
    dma = pltpu.SemaphoreType.DMA
    exchanged = pltpu.VMEM((n, rows // n, part), BF16)
    plain = pltpu.VMEM((rows, part), BF16)
    summed = pl.pallas_call(
        functools.partial(kernel, nx, nz),
        out_shape=jax.ShapeDtypeStruct((half, chans), F32),
        in_specs=[vmem] * 11,
        out_specs=vmem,
        scratch_shapes=[
            exchanged, exchanged,
            pltpu.VMEM((8, 128), BF16), pltpu.VMEM((half, part), BF16),
            exchanged, exchanged,
            plain, plain, plain,
            pltpu.VMEM((rows, part), F32),
            pltpu.VMEM((nx, groups, STRIDE, block, part), BF16),
            pltpu.VMEM((nx, groups, STRIDE, block, 2 * part + 128), BF16),
            pltpu.VMEM((nx, groups, STRIDE, block, part + 128), BF16),
            pltpu.VMEM((half, part), BF16), pltpu.VMEM((half, part), BF16),
            pltpu.VMEM((embed_table.shape[1] // 256, 256), F32),
            pltpu.VMEM((rows, rows), BF16), pltpu.VMEM((rows, rows), BF16), pltpu.VMEM((rows, rows), BF16),
            dma((n,)), dma((1,)), dma((n,)), dma((1,)),
            dma((2, hops)), dma((2, hops)), dma((2, 3)), dma((2, 3)), dma((2, nx - 1)), dma((2, nx - 1)),
            dma((4,)), dma((4,)), dma, dma, dma((2,)), dma((2,)),
        ],
        compiler_params=pltpu.CompilerParams(
            collective_id=0, has_side_effects=True, vmem_limit_bytes=56 * 2**20
        ),
    )(
        latents, spectrum.reshape(rows, part), w_value, w_gate, w_out, embed_table,
        prompt_ids.reshape(-1, 1), emb, cas_table(WW), cas_table(HH), cas_table(TT),
    )
    residual = lax.dynamic_slice_in_dim(latents, core * half, half, 0)
    return (residual.astype(F32) + summed).astype(BF16)


def solution(mesh):
    nx, nz = 4, mesh.shape["sp"] // 4
    torus = Mesh(
        mesh.devices.reshape(mesh.shape["grp"], nx, nz, mesh.shape["ch"]),
        ("grp", "sp_0", "sp_1", "ch"),
    )
    in_specs = (
        P(GRP_SP, None),
        P(None, None, SP, "ch"),
        P(SP, "ch"),
        P(SP, "ch"),
        P(SP, None),
        P(SP_CH, None),
        P("grp"),
        P("grp"),
    )
    out_specs = P(GRP_SP_CH, None)
    return jax.shard_map(
        functools.partial(local, nx, nz),
        mesh=torus, in_specs=in_specs, out_specs=out_specs, check_vma=False,
    )
```

time: 465 us -> 323 us (0.69)
  waiting for transfers between devices: 319 us -> 0 us
  Pallas kernels: 0 us -> 315 us
  blocking collectives: 50.3 us -> 0 us
  starting transfers between devices: 41.1 us -> 0 us
  matrix products: 18.7 us -> 0 us
  between operations: 14.6 us -> 0.67 us
  local copies, waits for them, and re-layouts: 13.9 us -> 1.48 us
    pallas_call x0 -> x1, Pallas kernels: none -> 315 us  [local(): pl.pallas_call(functools.partial(kernel, nx, nz), out_shape=jax.ShapeDtyp...]
    all_gather x3 -> x0, waiting for transfers between devices: 217 us -> none  [the longest x1 119 us: local(): column = lax.all_gather(packed, 'sp_1', axis=0, tiled=True)]
    all_to_all x2 -> x0, waiting for transfers between devices: 102 us -> none  [the longest x1 102 us: local(): lax.all_to_all(height_back.reshape(-1, lines, part), SP, split_axis=0, co...]
    unnamed x1 -> x0, blocking collectives: 43.6 us -> none
    all_to_all x2 -> x0, starting transfers between devices: 41 us -> none  [the longest x1 28.1 us: local(): lax.all_to_all(height_back.reshape(-1, lines, part), SP, split_axis=0, co...]
    dot_general x7 -> x0, matrix products: 18.7 us -> none  [the longest x4 16.7 us: dot(): return jnp.dot(a, b, preferred_element_type=F32)]
    convert_element_type x2 -> x0, local copies, waits for them, and re-layouts: 7.11 us -> none  [the longest x1 5.56 us: local(): space = space.reshape(TT * HH, TT * HH).astype(BF16)]
    all_to_all x1 -> x0, blocking collectives: 6.7 us -> none  [local(): moved = lax.all_to_all(mixed, 'ch', split_axis=0, concat_axis=1, tiled=True)]
  transfers between devices with their start and end apart: 5 -> 0, of which waited for: 4 -> 0; matrix products, arithmetic and copies ran while one was open for 3% -> 0% of each run, Pallas kernels for 0% -> 0%
where the time goes in v2:
time: 323 us; the launch traced here: 321 us
  Pallas kernels  315 us (98%)
  other arithmetic  3.59 us (1%)
    pallas_call x1, Pallas kernels, local(): pl.pallas_call(functools.partial(kernel, nx, nz), out_shape=jax.ShapeDtyp...  315 us

profile of v2, /device:TPU:33, one launch (start us, length us, event | category | flops | bytes accessed | tf_op | source)
XLA Modules:
  0.0 320.9 jit_solution(1991158537759340943)
XLA Ops:
  0.7 0.7 compare_select_fusion.emb
  1.3 1.5 copy.12.ids
  2.8 0.0 copy-start
  2.8 315.1 %shard_map.109 = f32[512,1024]{1,0:T(8,128)} custom-call(bf16[1024,1024]{1,0:T(8,128)(2,1)} %lat.1, bf16[1024,512]{1,0:T(8,128)(2,1)} %bitcast.3, bf16[8,512]{1,0:T(8,128)(2,1)} %wv_in.1, bf16[8,512]{1,0:T(8,128)(2,1)} %wg_in.1, bf16[8,1024]{1,0:T(8,128)(2,1)} %wo_in.1, bf16[4,32768]{1,0:T(4,128)(2,1)} %table.1, s32[256,1]{1,0:T(8,128)} %copy.12.ids, ...), custom_call_target="tpu_custom_call" | custom-call | tf_op jit(solution)/shard_map/pallas_call | solution.py:363
  317.9 0.0 copy-done
  317.9 2.9 add_convert_fusion
Async XLA Ops:
  2.8 315.1 %copy-start = (bf16[1024,1024]{1,0:T(8,128)(2,1)S(1)}, bf16[1024,1024]{1,0:T(8,128)(2,1)}, u32[]{:S(2)}) copy-start(bf16[1024,1024]{1,0:T(8,128)(2,1)} %lat.1) | copy-start | bytes 6291460

commit v3 on v2

--- a/solution.py
+++ b/solution.py
@@ -114,14 +114,14 @@
 
     pl.semaphore_wait(barrier, n)
 
+    bufs = (wv, wgo)
     groups = nz // STRIDE
     up = (groups + 1) // 2
     down = groups - 1 - up
 
     def hop(stream, direction, q):
-        buf = (wv, wgo)[stream]
         origin = (mz // STRIDE - direction * (q - 1) + groups) % groups
-        ref = buf.at[mx, origin, mz % STRIDE]
+        ref = bufs[stream].at[mx, origin, mz % STRIDE]
         k = (q - 1) if direction > 0 else up + q - 1
         return pltpu.make_async_remote_copy(
             src_ref=ref, dst_ref=ref,
@@ -130,9 +130,11 @@
         )
 
     def near(stream, k):
-        buf = (wv, wgo)[stream]
-        ref = buf.at[mx, :, mz % STRIDE]
-        step = (1, -1, 2)[k]
+        ref = bufs[stream].at[mx]
+        step = (1, -1, 1, -1)[k]
+        residue = (mz - (0, 0, 1, -1)[k] + nz) % STRIDE
+        part_of = (pl.ds(0, groups), pl.ds(0, groups), pl.ds(groups // 2, groups // 2), pl.ds(0, groups // 2))[k]
+        ref = ref.at[part_of, residue]
         return pltpu.make_async_remote_copy(
             src_ref=ref, dst_ref=ref,
             send_sem=r_send.at[stream, k], recv_sem=r_recv.at[stream, k],
@@ -140,19 +142,15 @@
         )
 
     def across(stream, k):
-        buf = (wv, wgo)[stream]
-        ref = buf.at[mx]
+        step = (1, -1, 1, -1)[k]
+        column = (mx - (0, 0, 1, -1)[k] + nx) % nx
+        part_of = (pl.ds(0, groups), pl.ds(0, groups), pl.ds(groups // 2, groups // 2), pl.ds(0, groups // 2))[k]
+        ref = bufs[stream].at[column, part_of]
         return pltpu.make_async_remote_copy(
             src_ref=ref, dst_ref=ref,
             send_sem=x_send.at[stream, k], recv_sem=x_recv.at[stream, k],
-            device_id={"sp_0": (mx + k + 1) % nx}, device_id_type=MESH,
+            device_id={"sp_0": (mx + step + nx) % nx}, device_id_type=MESH,
         )
-
-    def near_in(stream, k):
-        buf = (wv, wgo)[stream]
-        step = (1, -1, 2)[k]
-        ref = buf.at[mx, :, (mz - step + nz) % STRIDE]
-        return pltpu.make_async_copy(ref, ref, r_recv.at[stream, k])
 
     def gather_step(stream, step):
         if 0 < step <= up:
@@ -163,25 +161,26 @@
             hop(stream, 1, step + 1).start()
         if step < down:
             hop(stream, -1, step + 1).start()
-        if step == up:
-            for k in range(3):
-                near(stream, k).start()
-        if step == up + 1:
-            for k in range(3):
-                near_in(stream, k).wait()
-            for k in range(nx - 1):
-                across(stream, k).start()
-        if step == up + 2:
-            for k in range(nx - 1):
-                across(stream, k).wait_recv()
+        for first, copies in ((up, near), (up + 2, across)):
+            if step == first:
+                copies(stream, 0).start()
+                copies(stream, 1).start()
+            if step == first + 1:
+                copies(stream, 0).wait_recv()
+                copies(stream, 1).wait_recv()
+                copies(stream, 2).start()
+                copies(stream, 3).start()
+            if step == first + 2:
+                copies(stream, 2).wait_recv()
+                copies(stream, 3).wait_recv()
+        if step == up + 4:
             for q in range(up):
                 hop(stream, 1, q + 1).wait_send()
             for q in range(down):
                 hop(stream, -1, q + 1).wait_send()
-            for k in range(3):
-                near(stream, k).wait_send()
-            for k in range(nx - 1):
-                across(stream, k).wait_send()
+            for copies in (near, across):
+                for k in range(4):
+                    copies(stream, k).wait_send()
 
     def exchange(src, dst, send_sem, recv_sem):
         def copy(i):
@@ -221,11 +220,11 @@
     vocab = table.shape[1]
     low_count = 256
     high_count = vocab // low_count
-    prompt = ids.shape[0]
-    high_hot = one_hot(ids[...] // low_count == iota((prompt, high_count), 1))
-    low_hot = one_hot(ids[...] % low_count == iota((prompt, low_count), 1))
+    prompt = ids.shape[1]
+    high_hot = one_hot(ids[...] // low_count == iota((high_count, prompt), 0))
+    low_hot = one_hot(ids[...] % low_count == iota((low_count, prompt), 0))
     counts[...] = lax.dot_general(
-        high_hot, low_hot, (((0,), (0,)), ((), ())), preferred_element_type=F32
+        high_hot, low_hot, (((1,), (1,)), ((), ())), preferred_element_type=F32
     )
 
     def tally(h, total):
@@ -244,13 +243,17 @@
     terms = jnp.where(lane == 0, first, jnp.where(lane == 1, second, jnp.where(lane == 2, third, 0.0)))
     wgo[mx, mz // STRIDE, mz % STRIDE, :, 2 * part : 2 * part + 128] = terms.astype(BF16)
 
-    at = 8
-    total_steps = up + 3
-    for step in range(1, total_steps):
-        send(at, at + 8)
-        at += 8
-        gather_step(0, step)
-    gather_step(1, 0)
+    total_steps = up + 4
+
+    def send_beside(stream, first, last):
+        pace = (last - first) // total_steps
+        at = first
+        for step in range(1, total_steps + 1):
+            send(at, at + pace)
+            at += pace
+            gather_step(stream, step)
+        send(at, last)
+
     cells = TT * HH
     kt_wide = dot(kt[...], one_hot(iota((TT, cells), 1) // HH == iota((TT, cells), 0)))
     kh_wide = dot(kh[...], one_hot(iota((HH, cells), 1) % HH == iota((HH, cells), 0)))
@@ -260,17 +263,7 @@
     column_line = iota((WW, rows), 1) % lines
     for line in range(lines):
         wide[line * WW : (line + 1) * WW, :] = jnp.where(column_line == line, kw_wide, 0.0).astype(BF16)
-    for step in range(1, total_steps):
-        send(at, at + 8)
-        at += 8
-        gather_step(1, step)
-    upper = pl.ds(part, part + 128)
-    swap_out = pltpu.make_async_remote_copy(
-        src_ref=wgo.at[:, :, :, :, upper], dst_ref=wo_other, send_sem=o_send, recv_sem=o_recv,
-        device_id=other_core, device_id_type=MESH,
-    )
-    swap_out.start()
-    send(at, n - 1)
+    send_beside(0, 8, n - 1)
     drain()
 
     quarters = rows // tile
@@ -299,8 +292,15 @@
         ycopies[r].wait_send()
     returned[me] = back[me]
     send, drain = exchange(back, returned, b_send, b_recv)
-    send(0, n - 1)
-
+    gather_step(1, 0)
+    send_beside(1, 0, n - 1)
+
+    upper = pl.ds(part, part + 128)
+    swap_out = pltpu.make_async_remote_copy(
+        src_ref=wgo.at[:, :, :, :, upper], dst_ref=wo_other, send_sem=o_send, recv_sem=o_recv,
+        device_id=other_core, device_id_type=MESH,
+    )
+    swap_out.start()
     swap_out.wait()
     gathered = wgo.reshape(chans, 2 * part + 128)
     others = wo_other.reshape(chans, part + 128)
@@ -378,7 +378,7 @@
             pltpu.VMEM((embed_table.shape[1] // 256, 256), F32),
             pltpu.VMEM((rows, rows), BF16), pltpu.VMEM((rows, rows), BF16), pltpu.VMEM((rows, rows), BF16),
             dma((n,)), dma((1,)), dma((n,)), dma((1,)),
-            dma((2, hops)), dma((2, hops)), dma((2, 3)), dma((2, 3)), dma((2, nx - 1)), dma((2, nx - 1)),
+            dma((2, hops)), dma((2, hops)), dma((2, 4)), dma((2, 4)), dma((2, 4)), dma((2, 4)),
             dma((4,)), dma((4,)), dma, dma, dma((2,)), dma((2,)),
         ],
         compiler_params=pltpu.CompilerParams(
@@ -386,7 +386,7 @@
         ),
     )(
         latents, spectrum.reshape(rows, part), w_value, w_gate, w_out, embed_table,
-        prompt_ids.reshape(-1, 1), emb, cas_table(WW), cas_table(HH), cas_table(TT),
+        prompt_ids.reshape(1, -1), emb, cas_table(WW), cas_table(HH), cas_table(TT),
     )
     residual = lax.dynamic_slice_in_dim(latents, core * half, half, 0)
     return (residual.astype(F32) + summed).astype(BF16)

time: 323 us -> 299 us (0.926)
  Pallas kernels: 315 us -> 294 us
    pallas_call x1, Pallas kernels: 315 us -> 294 us  [local(): pl.pallas_call(functools.partial(kernel, nx, nz), out_shape=jax.ShapeDtyp...]
where the time goes in v3:
time: 299 us; the launch traced here: 298 us
  Pallas kernels  294 us (98%)
  other arithmetic  3.59 us (1%)
    pallas_call x1, Pallas kernels, local(): pl.pallas_call(functools.partial(kernel, nx, nz), out_shape=jax.ShapeDtyp...  294 us

profile of v3, /device:TPU:33, one launch (start us, length us, event | category | flops | bytes accessed | tf_op | source)
XLA Modules:
  0.0 298.4 jit_solution(5706983832610405797)
XLA Ops:
  0.7 0.7 compare_select_fusion.emb
  1.3 0.0 copy-start
  1.3 294.1 %shard_map.109 = f32[512,1024]{1,0:T(8,128)} custom-call(bf16[1024,1024]{1,0:T(8,128)(2,1)} %lat.1, bf16[1024,512]{1,0:T(8,128)(2,1)} %bitcast.3, bf16[8,512]{1,0:T(8,128)(2,1)} %wv_in.1, bf16[8,512]{1,0:T(8,128)(2,1)} %wg_in.1, bf16[8,1024]{1,0:T(8,128)(2,1)} %wo_in.1, bf16[4,32768]{1,0:T(4,128)(2,1)} %table.1, s32[1,256]{1,0:T(1,128)} %bitcast.4, ...), custom_call_target="tpu_custom_call" | custom-call | tf_op jit(solution)/shard_map/pallas_call | solution.py:363
  295.4 0.0 copy-done
  295.4 2.9 add_convert_fusion
Async XLA Ops:
  1.3 294.1 %copy-start = (bf16[1024,1024]{1,0:T(8,128)(2,1)S(1)}, bf16[1024,1024]{1,0:T(8,128)(2,1)}, u32[]{:S(2)}) copy-start(bf16[1024,1024]{1,0:T(8,128)(2,1)} %lat.1) | copy-start | bytes 6291460

commit v4 on v3

--- a/solution.py
+++ b/solution.py
@@ -58,8 +58,8 @@
     lat, spec, wv_in, wg_in, wo_in, table, ids, emb, kw, kh, kt,
     out,
     spread, arrived, spin, spout, back, returned, y_own, y_other, filt, gain,
-    wv, wgo, wo_other, mix_own, mix_other, counts, space, wide, narrow,
-    a_send, a_recv, b_send, b_recv, s_send, s_recv, r_send, r_recv, x_send, x_recv,
+    wall, wo_other, mix_own, mix_other, counts, space, wide, narrow,
+    hello, a_send, a_recv, b_send, b_recv, s_send, s_recv, r_send, r_recv,
     y_send, y_recv, o_send, o_recv, m_send, m_recv,
 ):
     n = nx * nz
@@ -79,15 +79,36 @@
         tx, tz = (mx + dx) % nx, (mz + dz) % nz
         return {"sp_0": tx, "sp_1": tz}, tx * nz + tz
 
+    def layered(i):
+        tx, tz = (mx + i % nx) % nx, i // nx
+        return {"sp_0": tx, "sp_1": tz}, tx * nz + tz
+
     barrier = pltpu.get_barrier_semaphore()
-
-    def greet(i, carry):
-        device, _ = partner(i)
+    for dx in range(1, nx):
+        pl.semaphore_signal(
+            barrier, inc=1, device_id={"sp_0": (mx + dx) % nx}, device_id_type=MESH
+        )
+    pl.semaphore_signal(barrier, inc=1, device_id=other_core, device_id_type=MESH)
+    pl.semaphore_wait(barrier, jnp.where(mz > 0, 2 * nx, nx))
+
+    def tell(dx, carry):
+        device = {"sp_0": (mx + dx) % nx, "sp_1": mz + 1}
         pl.semaphore_signal(barrier, inc=1, device_id=device, device_id_type=MESH)
         return carry
 
-    lax.fori_loop(0, n - 1, greet, 0)
-    pl.semaphore_signal(barrier, inc=1, device_id=other_core, device_id_type=MESH)
+    lax.fori_loop(0, jnp.where(mz < nz - 1, nx, 0), tell, 0)
+
+    def greet(i, carry):
+        device, _ = layered(i)
+        pl.semaphore_signal(hello.at[mz], inc=1, device_id=device, device_id_type=MESH)
+        return carry
+
+    lax.fori_loop(0, nx * mz, greet, 0)
+
+    def hear(layer):
+        @pl.when(layer > mz)
+        def _():
+            pl.semaphore_wait(hello.at[layer], nx)
 
     pick = one_hot(iota((rows, WW), 0) // lines == iota((rows, WW), 1))
     spread_rows = dot(pick, kw[...]).astype(BF16)
@@ -108,114 +129,100 @@
 
     lax.fori_loop(0, rows // tile, widen, 0)
     arrived[me] = spread[me]
-    wv[mx, mz // STRIDE, mz % STRIDE] = wv_in[...]
-    wgo[mx, mz // STRIDE, mz % STRIDE, :, 0:part] = wg_in[...]
-    wgo[mx, mz // STRIDE, mz % STRIDE, :, part : 2 * part] = wo_in[:, mine]
-
-    pl.semaphore_wait(barrier, n)
-
-    bufs = (wv, wgo)
+    wall[mx, mz // STRIDE, mz % STRIDE, :, 0:part] = wv_in[...]
+    wall[mx, mz // STRIDE, mz % STRIDE, :, part : 2 * part] = wg_in[...]
+    wall[mx, mz // STRIDE, mz % STRIDE, :, 2 * part : 3 * part] = wo_in[:, mine]
+
     groups = nz // STRIDE
     up = (groups + 1) // 2
     down = groups - 1 - up
 
-    def hop(stream, direction, q):
+    first_part = pl.ds(0, part)
+    later_part = pl.ds(part, 2 * part + 128)
+
+    def hop(direction, q):
         origin = (mz // STRIDE - direction * (q - 1) + groups) % groups
-        ref = bufs[stream].at[mx, origin, mz % STRIDE]
+        ref = wall.at[mx, origin, mz % STRIDE]
         k = (q - 1) if direction > 0 else up + q - 1
         return pltpu.make_async_remote_copy(
-            src_ref=ref, dst_ref=ref,
-            send_sem=s_send.at[stream, k], recv_sem=s_recv.at[stream, k],
+            src_ref=ref, dst_ref=ref, send_sem=s_send.at[k], recv_sem=s_recv.at[k],
             device_id={"sp_1": (mz + direction * STRIDE + nz) % nz}, device_id_type=MESH,
         )
 
-    def near(stream, k):
-        ref = bufs[stream].at[mx]
+    def hop_in(q):
+        hop(1, q).wait_recv()
+        if q <= down:
+            hop(-1, q).wait_recv()
+
+    def hop_out(q):
+        hop(1, q).start()
+        if q <= down:
+            hop(-1, q).start()
+
+    def group_span(k):
+        return ((0, groups), (0, groups), (groups // 2, groups), (0, groups // 2))[k]
+
+    def piece(stage, k, g, count):
         step = (1, -1, 1, -1)[k]
-        residue = (mz - (0, 0, 1, -1)[k] + nz) % STRIDE
-        part_of = (pl.ds(0, groups), pl.ds(0, groups), pl.ds(groups // 2, groups // 2), pl.ds(0, groups // 2))[k]
-        ref = ref.at[part_of, residue]
+        back_by = (0, 0, 1, -1)[k]
+        if stage:
+            lanes = (first_part, later_part)[stage - 1]
+            ref = wall.at[(mx - back_by + nx) % nx, pl.ds(g, count), :, :, lanes]
+            device = {"sp_0": (mx + step + nx) % nx}
+        else:
+            ref = wall.at[mx, pl.ds(g, count), (mz - back_by + nz) % STRIDE]
+            device = {"sp_1": (mz + step + nz) % nz}
         return pltpu.make_async_remote_copy(
-            src_ref=ref, dst_ref=ref,
-            send_sem=r_send.at[stream, k], recv_sem=r_recv.at[stream, k],
-            device_id={"sp_1": (mz + step + nz) % nz}, device_id_type=MESH,
+            src_ref=ref, dst_ref=ref, send_sem=r_send.at[stage, k], recv_sem=r_recv.at[stage, k],
+            device_id=device, device_id_type=MESH,
         )
 
-    def across(stream, k):
-        step = (1, -1, 1, -1)[k]
-        column = (mx - (0, 0, 1, -1)[k] + nx) % nx
-        part_of = (pl.ds(0, groups), pl.ds(0, groups), pl.ds(groups // 2, groups // 2), pl.ds(0, groups // 2))[k]
-        ref = bufs[stream].at[column, part_of]
-        return pltpu.make_async_remote_copy(
-            src_ref=ref, dst_ref=ref,
-            send_sem=x_send.at[stream, k], recv_sem=x_recv.at[stream, k],
-            device_id={"sp_0": (mx + step + nx) % nx}, device_id_type=MESH,
-        )
-
-    def gather_step(stream, step):
-        if 0 < step <= up:
-            hop(stream, 1, step).wait_recv()
-        if 0 < step <= down:
-            hop(stream, -1, step).wait_recv()
-        if step < up:
-            hop(stream, 1, step + 1).start()
-        if step < down:
-            hop(stream, -1, step + 1).start()
-        for first, copies in ((up, near), (up + 2, across)):
-            if step == first:
-                copies(stream, 0).start()
-                copies(stream, 1).start()
-            if step == first + 1:
-                copies(stream, 0).wait_recv()
-                copies(stream, 1).wait_recv()
-                copies(stream, 2).start()
-                copies(stream, 3).start()
-            if step == first + 2:
-                copies(stream, 2).wait_recv()
-                copies(stream, 3).wait_recv()
-        if step == up + 4:
-            for q in range(up):
-                hop(stream, 1, q + 1).wait_send()
-            for q in range(down):
-                hop(stream, -1, q + 1).wait_send()
-            for copies in (near, across):
-                for k in range(4):
-                    copies(stream, k).wait_send()
-
-    def exchange(src, dst, send_sem, recv_sem):
+    def whole(stage, k):
+        low, high = group_span(k)
+        return piece(stage, k, low, high - low)
+
+    def exchange(src, dst, send_sem, recv_sem, layers):
+        count = n if layers else n - 1
+
         def copy(i):
-            device, target = partner(i)
+            device, target = layered(i) if layers else partner(i)
             return pltpu.make_async_remote_copy(
                 src_ref=src.at[target], dst_ref=dst.at[me],
                 send_sem=send_sem.at[i], recv_sem=recv_sem.at[0],
                 device_id=device, device_id_type=MESH,
             )
 
-        def send(first, last):
+        def there(i, do):
+            if layers:
+                pl.when(i != mz * nx)(do)
+            else:
+                do()
+
+        def send(first, last, listen=False):
             def body(i, carry):
                 @pl.when(i >= WINDOW)
                 def _():
-                    copy(i - WINDOW).wait_send()
-
-                copy(i).start()
+                    there(i - WINDOW, lambda: copy(i - WINDOW).wait_send())
+
+                if listen:
+                    pl.when(i % nx == 0)(lambda: hear(i // nx))
+                there(i, lambda: copy(i).start())
                 return carry
 
             lax.fori_loop(first, last, body, 0)
 
         def drain():
             def body(i, carry):
-                copy(i).wait_send()
+                there(i, lambda: copy(i).wait_send())
                 return carry
 
-            lax.fori_loop(n - 1 - WINDOW, n - 1, body, 0)
+            lax.fori_loop(count - WINDOW, count, body, 0)
             some = dst.at[pl.ds(0, n - 1)]
             pltpu.make_async_copy(some, some, recv_sem.at[0]).wait()
 
         return send, drain
 
-    send, drain = exchange(spread, arrived, a_send, a_recv)
-    gather_step(0, 0)
-    send(0, 8)
+    send, drain = exchange(spread, arrived, a_send, a_recv, True)
 
     vocab = table.shape[1]
     low_count = 256
@@ -241,18 +248,35 @@
     third = pooled8 - first - second
     lane = iota((block, 128), 1)
     terms = jnp.where(lane == 0, first, jnp.where(lane == 1, second, jnp.where(lane == 2, third, 0.0)))
-    wgo[mx, mz // STRIDE, mz % STRIDE, :, 2 * part : 2 * part + 128] = terms.astype(BF16)
-
-    total_steps = up + 4
-
-    def send_beside(stream, first, last):
-        pace = (last - first) // total_steps
-        at = first
-        for step in range(1, total_steps + 1):
-            send(at, at + pace)
-            at += pace
-            gather_step(stream, step)
-        send(at, last)
+    wall[mx, mz // STRIDE, mz % STRIDE, :, 3 * part : 3 * part + 128] = terms.astype(BF16)
+
+    heard = nz - 4 - (mz * (nz - 5)) // nz
+    send(0, heard * nx, True)
+
+    def hear_rest(layer, carry):
+        hear(layer)
+        return carry
+
+    lax.fori_loop(heard, nz, hear_rest, 0)
+    hop_out(1)
+
+    def send_pieces(stage, at, each, slack):
+        for pair in ((0, 1), (2, 3)):
+            count = group_span(pair[0])[1] - group_span(pair[0])[0]
+
+            def body(g, carry, at=at, pair=pair):
+                for k in pair:
+                    piece(stage, k, group_span(k)[0] + g, 1).start()
+                send(at + g * each, at + (g + 1) * each)
+                return carry
+
+            lax.fori_loop(0, count, body, 0)
+            at += count * each
+            send(at, at + slack)
+            at += slack
+            for k in pair:
+                whole(stage, k).wait_recv()
+        return at
 
     cells = TT * HH
     kt_wide = dot(kt[...], one_hot(iota((TT, cells), 1) // HH == iota((TT, cells), 0)))
@@ -263,7 +287,35 @@
     column_line = iota((WW, rows), 1) % lines
     for line in range(lines):
         wide[line * WW : (line + 1) * WW, :] = jnp.where(column_line == line, kw_wide, 0.0).astype(BF16)
-    send_beside(0, 8, n - 1)
+    begin = heard * nx
+    left_over = n - begin
+
+    def until(share):
+        return begin + left_over * share // 128
+
+    done = begin
+    for q in range(1, up + 1):
+        send(done, until(11 * q))
+        done = until(11 * q)
+        hop_in(q)
+        if q < up:
+            hop_out(q + 1)
+    share = 11 * up
+    for stage in (0, 1):
+        for pair in ((0, 1), (2, 3)):
+            count = group_span(pair[0])[1] - group_span(pair[0])[0]
+            for g in range(count):
+                for k in pair:
+                    piece(stage, k, group_span(k)[0] + g, 1).start()
+                share += 1
+                send(done, until(share))
+                done = until(share)
+            share += 7
+            send(done, until(share))
+            done = until(share)
+            for k in pair:
+                whole(stage, k).wait_recv()
+    send(done, n)
     drain()
 
     quarters = rows // tile
@@ -277,7 +329,8 @@
             send_sem=y_send.at[r], recv_sem=y_recv.at[r], device_id=other_core, device_id_type=MESH,
         ))
         ycopies[-1].start()
-    weight = wv.reshape(chans, part)
+    gathered = wall.reshape(chans, 3 * part + 128)
+    weight = gathered.at[:, 0:part]
     own_rows = pl.ds(pl.multiple_of(core * part, part), part)
     other_rows = pl.ds(pl.multiple_of((1 - core) * part, part), part)
     for r in range(quarters):
@@ -291,27 +344,33 @@
         back[r * per : (r + 1) * per] = got.reshape(per, block, part)
         ycopies[r].wait_send()
     returned[me] = back[me]
-    send, drain = exchange(back, returned, b_send, b_recv)
-    gather_step(1, 0)
-    send_beside(1, 0, n - 1)
-
-    upper = pl.ds(part, part + 128)
+    send, drain = exchange(back, returned, b_send, b_recv, False)
+    at = send_pieces(2, 0, 6, 16)
+    send(at, n - 1)
+    for q in range(1, up + 1):
+        hop(1, q).wait_send()
+        if q <= down:
+            hop(-1, q).wait_send()
+    for stage in range(3):
+        for k in range(4):
+            whole(stage, k).wait_send()
+
+    upper = pl.ds(2 * part, part + 128)
     swap_out = pltpu.make_async_remote_copy(
-        src_ref=wgo.at[:, :, :, :, upper], dst_ref=wo_other, send_sem=o_send, recv_sem=o_recv,
+        src_ref=wall.at[:, :, :, :, upper], dst_ref=wo_other, send_sem=o_send, recv_sem=o_recv,
         device_id=other_core, device_id_type=MESH,
     )
     swap_out.start()
     swap_out.wait()
-    gathered = wgo.reshape(chans, 2 * part + 128)
     others = wo_other.reshape(chans, part + 128)
-    pools = gathered[:, 2 * part : 2 * part + 128] + others[:, part : part + 128]
+    pools = gathered[:, 3 * part : 3 * part + 128] + others[:, part : part + 128]
     chosen = one_hot(iota((chans, part), 0) == iota((chans, part), 1) + core * part)
     terms = lax.dot_general(pools, chosen, (((0,), (0,)), ((), ())), preferred_element_type=F32)
     modulation = 1.0 + jnp.sum(terms[0:8, :], axis=0, keepdims=True) + emb[...]
 
     def gate(r, carry):
         here = pl.ds(pl.multiple_of(r * tile, tile), tile)
-        v = dot(lat[here, :], gathered[:, 0:part])
+        v = dot(lat[here, :], gathered[:, part : 2 * part])
         gain[here, :] = v / (1.0 + jnp.exp(-v)) * modulation
         return carry
 
@@ -340,7 +399,7 @@
     for r in range(half // tile):
         here = slice(r * tile, (r + 1) * tile)
         mcopies[r].wait()
-        for at, weight in ((left, gathered.at[:, part : 2 * part]), (right, others.at[:, 0:part])):
+        for at, weight in ((left, gathered.at[:, 2 * part : 3 * part]), (right, others.at[:, 0:part])):
             out[here, at] = dot(mix_own[here, :], weight[own_rows, :]) + dot(
                 mix_other[here, :], weight[other_rows, :]
             )
@@ -371,14 +430,13 @@
             exchanged, exchanged,
             plain, plain, plain,
             pltpu.VMEM((rows, part), F32),
-            pltpu.VMEM((nx, groups, STRIDE, block, part), BF16),
-            pltpu.VMEM((nx, groups, STRIDE, block, 2 * part + 128), BF16),
+            pltpu.VMEM((nx, groups, STRIDE, block, 3 * part + 128), BF16),
             pltpu.VMEM((nx, groups, STRIDE, block, part + 128), BF16),
             pltpu.VMEM((half, part), BF16), pltpu.VMEM((half, part), BF16),
             pltpu.VMEM((embed_table.shape[1] // 256, 256), F32),
             pltpu.VMEM((rows, rows), BF16), pltpu.VMEM((rows, rows), BF16), pltpu.VMEM((rows, rows), BF16),
-            dma((n,)), dma((1,)), dma((n,)), dma((1,)),
-            dma((2, hops)), dma((2, hops)), dma((2, 4)), dma((2, 4)), dma((2, 4)), dma((2, 4)),
+            pltpu.SemaphoreType.REGULAR((nz,)), dma((n,)), dma((1,)), dma((n,)), dma((1,)),
+            dma((hops,)), dma((hops,)), dma((3, 4)), dma((3, 4)),
             dma((4,)), dma((4,)), dma, dma, dma((2,)), dma((2,)),
         ],
         compiler_params=pltpu.CompilerParams(

time: 299 us -> 430 us (1.44)
  Pallas kernels: 294 us -> 426 us
    pallas_call x1, Pallas kernels: 294 us -> 426 us  [local(): pl.pallas_call(functools.partial(kernel, nx, nz), out_shape=jax.ShapeDtyp...]
where the time goes in v4:
time: 430 us
  Pallas kernels  426 us (99%)
    pallas_call x1, Pallas kernels, local(): pl.pallas_call(functools.partial(kernel, nx, nz), out_shape=jax.ShapeDtyp...  426 us

profile of v4, /device:TPU:33, one launch (start us, length us, event | category | flops | bytes accessed | tf_op | source)
XLA Modules:
  0.0 430.1 jit_solution(15244975303267031701)
XLA Ops:
  0.7 0.7 compare_select_fusion.emb
  1.3 0.0 copy-start
  1.3 425.8 %shard_map.109 = f32[512,1024]{1,0:T(8,128)} custom-call(bf16[1024,1024]{1,0:T(8,128)(2,1)} %lat.1, bf16[1024,512]{1,0:T(8,128)(2,1)} %bitcast.3, bf16[8,512]{1,0:T(8,128)(2,1)} %wv_in.1, bf16[8,512]{1,0:T(8,128)(2,1)} %wg_in.1, bf16[8,1024]{1,0:T(8,128)(2,1)} %wo_in.1, bf16[4,32768]{1,0:T(4,128)(2,1)} %table.1, s32[1,256]{1,0:T(1,128)} %bitcast.4, ...), custom_call_target="tpu_custom_call" | custom-call | tf_op jit(solution)/shard_map/pallas_call | solution.py:422
  427.2 0.0 copy-done
  427.2 2.9 add_convert_fusion
Async XLA Ops:
  1.3 425.8 %copy-start = (bf16[1024,1024]{1,0:T(8,128)(2,1)S(1)}, bf16[1024,1024]{1,0:T(8,128)(2,1)}, u32[]{:S(2)}) copy-start(bf16[1024,1024]{1,0:T(8,128)(2,1)} %lat.1) | copy-start | bytes 6291460

commit v5 on v4

--- a/solution.py
+++ b/solution.py
@@ -59,7 +59,7 @@
     out,
     spread, arrived, spin, spout, back, returned, y_own, y_other, filt, gain,
     wall, wo_other, mix_own, mix_other, counts, space, wide, narrow,
-    hello, a_send, a_recv, b_send, b_recv, s_send, s_recv, r_send, r_recv,
+    hello, ring_hello, a_send, a_recv, b_send, b_recv, s_send, s_recv, r_send, r_recv,
     y_send, y_recv, o_send, o_recv, m_send, m_recv,
 ):
     n = nx * nz
@@ -79,9 +79,8 @@
         tx, tz = (mx + dx) % nx, (mz + dz) % nz
         return {"sp_0": tx, "sp_1": tz}, tx * nz + tz
 
-    def layered(i):
-        tx, tz = (mx + i % nx) % nx, i // nx
-        return {"sp_0": tx, "sp_1": tz}, tx * nz + tz
+    def below(i):
+        return {"sp_0": (mx + i % nx) % nx, "sp_1": i // nx}
 
     barrier = pltpu.get_barrier_semaphore()
     for dx in range(1, nx):
@@ -99,8 +98,7 @@
     lax.fori_loop(0, jnp.where(mz < nz - 1, nx, 0), tell, 0)
 
     def greet(i, carry):
-        device, _ = layered(i)
-        pl.semaphore_signal(hello.at[mz], inc=1, device_id=device, device_id_type=MESH)
+        pl.semaphore_signal(hello.at[mz], inc=1, device_id=below(i), device_id_type=MESH)
         return carry
 
     lax.fori_loop(0, nx * mz, greet, 0)
@@ -109,6 +107,17 @@
         @pl.when(layer > mz)
         def _():
             pl.semaphore_wait(hello.at[layer], nx)
+
+    ring_steps = (1, -1, STRIDE, -STRIDE)
+    above = 0
+    for step in ring_steps:
+        layer = (mz + step + nz) % nz
+
+        @pl.when(layer < mz)
+        def _():
+            pl.semaphore_signal(ring_hello, inc=1, device_id={"sp_1": layer}, device_id_type=MESH)
+
+        above = above + jnp.where(layer > mz, 1, 0)
 
     pick = one_hot(iota((rows, WW), 0) // lines == iota((rows, WW), 1))
     spread_rows = dot(pick, kw[...]).astype(BF16)
@@ -181,42 +190,39 @@
         low, high = group_span(k)
         return piece(stage, k, low, high - low)
 
-    def exchange(src, dst, send_sem, recv_sem, layers):
-        count = n if layers else n - 1
-
+    def exchange(src, dst, send_sem, recv_sem, listen):
         def copy(i):
-            device, target = layered(i) if layers else partner(i)
+            device, target = partner(i)
             return pltpu.make_async_remote_copy(
                 src_ref=src.at[target], dst_ref=dst.at[me],
                 send_sem=send_sem.at[i], recv_sem=recv_sem.at[0],
                 device_id=device, device_id_type=MESH,
             )
 
-        def there(i, do):
-            if layers:
-                pl.when(i != mz * nx)(do)
-            else:
-                do()
-
-        def send(first, last, listen=False):
+        def send(first, last):
             def body(i, carry):
                 @pl.when(i >= WINDOW)
                 def _():
-                    there(i - WINDOW, lambda: copy(i - WINDOW).wait_send())
+                    copy(i - WINDOW).wait_send()
 
                 if listen:
-                    pl.when(i % nx == 0)(lambda: hear(i // nx))
-                there(i, lambda: copy(i).start())
+
+                    @pl.when(i % nx == 0)
+                    def _():
+                        _, target = partner(i)
+                        hear(target % nz)
+
+                copy(i).start()
                 return carry
 
             lax.fori_loop(first, last, body, 0)
 
         def drain():
             def body(i, carry):
-                there(i, lambda: copy(i).wait_send())
+                copy(i).wait_send()
                 return carry
 
-            lax.fori_loop(count - WINDOW, count, body, 0)
+            lax.fori_loop(n - 1 - WINDOW, n - 1, body, 0)
             some = dst.at[pl.ds(0, n - 1)]
             pltpu.make_async_copy(some, some, recv_sem.at[0]).wait()
 
@@ -250,14 +256,9 @@
     terms = jnp.where(lane == 0, first, jnp.where(lane == 1, second, jnp.where(lane == 2, third, 0.0)))
     wall[mx, mz // STRIDE, mz % STRIDE, :, 3 * part : 3 * part + 128] = terms.astype(BF16)
 
-    heard = nz - 4 - (mz * (nz - 5)) // nz
-    send(0, heard * nx, True)
-
-    def hear_rest(layer, carry):
-        hear(layer)
-        return carry
-
-    lax.fori_loop(heard, nz, hear_rest, 0)
+    begin = jnp.where(mz < STRIDE, 28, 8)
+    send(0, begin)
+    pl.when(above > 0)(lambda: pl.semaphore_wait(ring_hello, above))
     hop_out(1)
 
     def send_pieces(stage, at, each, slack):
@@ -287,8 +288,7 @@
     column_line = iota((WW, rows), 1) % lines
     for line in range(lines):
         wide[line * WW : (line + 1) * WW, :] = jnp.where(column_line == line, kw_wide, 0.0).astype(BF16)
-    begin = heard * nx
-    left_over = n - begin
+    left_over = n - 1 - begin
 
     def until(share):
         return begin + left_over * share // 128
@@ -315,7 +315,7 @@
             done = until(share)
             for k in pair:
                 whole(stage, k).wait_recv()
-    send(done, n)
+    send(done, n - 1)
     drain()
 
     quarters = rows // tile
@@ -435,7 +435,7 @@
             pltpu.VMEM((half, part), BF16), pltpu.VMEM((half, part), BF16),
             pltpu.VMEM((embed_table.shape[1] // 256, 256), F32),
             pltpu.VMEM((rows, rows), BF16), pltpu.VMEM((rows, rows), BF16), pltpu.VMEM((rows, rows), BF16),
-            pltpu.SemaphoreType.REGULAR((nz,)), dma((n,)), dma((1,)), dma((n,)), dma((1,)),
+            pltpu.SemaphoreType.REGULAR((nz,)), pltpu.SemaphoreType.REGULAR, dma((n,)), dma((1,)), dma((n,)), dma((1,)),
             dma((hops,)), dma((hops,)), dma((3, 4)), dma((3, 4)),
             dma((4,)), dma((4,)), dma, dma, dma((2,)), dma((2,)),
         ],

time: 430 us -> 343 us (0.80)
  Pallas kernels: 426 us -> 338 us
    pallas_call x1, Pallas kernels: 426 us -> 338 us  [local(): pl.pallas_call(functools.partial(kernel, nx, nz), out_shape=jax.ShapeDtyp...]
where the time goes in v5:
time: 343 us; the launch traced here: 342 us
  Pallas kernels  338 us (99%)
  other arithmetic  3.59 us (1%)
    pallas_call x1, Pallas kernels, local(): pl.pallas_call(functools.partial(kernel, nx, nz), out_shape=jax.ShapeDtyp...  338 us

profile of v5, /device:TPU:33, one launch (start us, length us, event | category | flops | bytes accessed | tf_op | source)
XLA Modules:
  0.0 342.3 jit_solution(13517269611038306238)
XLA Ops:
  0.7 0.7 compare_select_fusion.emb
  1.3 0.0 copy-start
  1.3 338.1 %shard_map.109 = f32[512,1024]{1,0:T(8,128)} custom-call(bf16[1024,1024]{1,0:T(8,128)(2,1)} %lat.1, bf16[1024,512]{1,0:T(8,128)(2,1)} %bitcast.3, bf16[8,512]{1,0:T(8,128)(2,1)} %wv_in.1, bf16[8,512]{1,0:T(8,128)(2,1)} %wg_in.1, bf16[8,1024]{1,0:T(8,128)(2,1)} %wo_in.1, bf16[4,32768]{1,0:T(4,128)(2,1)} %table.1, s32[1,256]{1,0:T(1,128)} %bitcast.4, ...), custom_call_target="tpu_custom_call" | custom-call | tf_op jit(solution)/shard_map/pallas_call | solution.py:422
  339.4 0.0 copy-done
  339.4 2.9 add_convert_fusion
Async XLA Ops:
  1.3 338.1 %copy-start = (bf16[1024,1024]{1,0:T(8,128)(2,1)S(1)}, bf16[1024,1024]{1,0:T(8,128)(2,1)}, u32[]{:S(2)}) copy-start(bf16[1024,1024]{1,0:T(8,128)(2,1)} %lat.1) | copy-start | bytes 6291460

commit v6 on v5

--- a/solution.py
+++ b/solution.py
@@ -21,7 +21,7 @@
 BF16 = jnp.bfloat16
 MESH = pl.DeviceIdType.MESH
 STRIDE = 4
-WINDOW = 16
+WINDOW = 40
 
 
 def cas_table(length):
@@ -59,7 +59,7 @@
     out,
     spread, arrived, spin, spout, back, returned, y_own, y_other, filt, gain,
     wall, wo_other, mix_own, mix_other, counts, space, wide, narrow,
-    hello, ring_hello, a_send, a_recv, b_send, b_recv, s_send, s_recv, r_send, r_recv,
+    a_send, a_recv, b_send, b_recv, s_send, s_recv, r_send, r_recv,
     y_send, y_recv, o_send, o_recv, m_send, m_recv,
 ):
     n = nx * nz
@@ -79,45 +79,15 @@
         tx, tz = (mx + dx) % nx, (mz + dz) % nz
         return {"sp_0": tx, "sp_1": tz}, tx * nz + tz
 
-    def below(i):
-        return {"sp_0": (mx + i % nx) % nx, "sp_1": i // nx}
-
     barrier = pltpu.get_barrier_semaphore()
-    for dx in range(1, nx):
-        pl.semaphore_signal(
-            barrier, inc=1, device_id={"sp_0": (mx + dx) % nx}, device_id_type=MESH
-        )
-    pl.semaphore_signal(barrier, inc=1, device_id=other_core, device_id_type=MESH)
-    pl.semaphore_wait(barrier, jnp.where(mz > 0, 2 * nx, nx))
-
-    def tell(dx, carry):
-        device = {"sp_0": (mx + dx) % nx, "sp_1": mz + 1}
+
+    def greet(i, carry):
+        device, _ = partner(i)
         pl.semaphore_signal(barrier, inc=1, device_id=device, device_id_type=MESH)
         return carry
 
-    lax.fori_loop(0, jnp.where(mz < nz - 1, nx, 0), tell, 0)
-
-    def greet(i, carry):
-        pl.semaphore_signal(hello.at[mz], inc=1, device_id=below(i), device_id_type=MESH)
-        return carry
-
-    lax.fori_loop(0, nx * mz, greet, 0)
-
-    def hear(layer):
-        @pl.when(layer > mz)
-        def _():
-            pl.semaphore_wait(hello.at[layer], nx)
-
-    ring_steps = (1, -1, STRIDE, -STRIDE)
-    above = 0
-    for step in ring_steps:
-        layer = (mz + step + nz) % nz
-
-        @pl.when(layer < mz)
-        def _():
-            pl.semaphore_signal(ring_hello, inc=1, device_id={"sp_1": layer}, device_id_type=MESH)
-
-        above = above + jnp.where(layer > mz, 1, 0)
+    lax.fori_loop(0, n - 1, greet, 0)
+    pl.semaphore_signal(barrier, inc=1, device_id=other_core, device_id_type=MESH)
 
     pick = one_hot(iota((rows, WW), 0) // lines == iota((rows, WW), 1))
     spread_rows = dot(pick, kw[...]).astype(BF16)
@@ -142,6 +112,8 @@
     wall[mx, mz // STRIDE, mz % STRIDE, :, part : 2 * part] = wg_in[...]
     wall[mx, mz // STRIDE, mz % STRIDE, :, 2 * part : 3 * part] = wo_in[:, mine]
 
+    pl.semaphore_wait(barrier, n)
+
     groups = nz // STRIDE
     up = (groups + 1) // 2
     down = groups - 1 - up
@@ -149,24 +121,24 @@
     first_part = pl.ds(0, part)
     later_part = pl.ds(part, 2 * part + 128)
 
-    def hop(direction, q):
+    def hop(stream, direction, q):
         origin = (mz // STRIDE - direction * (q - 1) + groups) % groups
-        ref = wall.at[mx, origin, mz % STRIDE]
+        ref = wall.at[mx, origin, mz % STRIDE, :, (first_part, later_part)[stream]]
         k = (q - 1) if direction > 0 else up + q - 1
         return pltpu.make_async_remote_copy(
-            src_ref=ref, dst_ref=ref, send_sem=s_send.at[k], recv_sem=s_recv.at[k],
+            src_ref=ref, dst_ref=ref, send_sem=s_send.at[stream, k], recv_sem=s_recv.at[stream, k],
             device_id={"sp_1": (mz + direction * STRIDE + nz) % nz}, device_id_type=MESH,
         )
 
-    def hop_in(q):
-        hop(1, q).wait_recv()
+    def hop_in(stream, q):
+        hop(stream, 1, q).wait_recv()
         if q <= down:
-            hop(-1, q).wait_recv()
-
-    def hop_out(q):
-        hop(1, q).start()
+            hop(stream, -1, q).wait_recv()
+
+    def hop_out(stream, q):
+        hop(stream, 1, q).start()
         if q <= down:
-            hop(-1, q).start()
+            hop(stream, -1, q).start()
 
     def group_span(k):
         return ((0, groups), (0, groups), (groups // 2, groups), (0, groups // 2))[k]
@@ -174,12 +146,12 @@
     def piece(stage, k, g, count):
         step = (1, -1, 1, -1)[k]
         back_by = (0, 0, 1, -1)[k]
-        if stage:
-            lanes = (first_part, later_part)[stage - 1]
+        lanes = (first_part, later_part)[stage // 2]
+        if stage % 2:
             ref = wall.at[(mx - back_by + nx) % nx, pl.ds(g, count), :, :, lanes]
             device = {"sp_0": (mx + step + nx) % nx}
         else:
-            ref = wall.at[mx, pl.ds(g, count), (mz - back_by + nz) % STRIDE]
+            ref = wall.at[mx, pl.ds(g, count), (mz - back_by + nz) % STRIDE, :, lanes]
             device = {"sp_1": (mz + step + nz) % nz}
         return pltpu.make_async_remote_copy(
             src_ref=ref, dst_ref=ref, send_sem=r_send.at[stage, k], recv_sem=r_recv.at[stage, k],
@@ -190,7 +162,7 @@
         low, high = group_span(k)
         return piece(stage, k, low, high - low)
 
-    def exchange(src, dst, send_sem, recv_sem, listen):
+    def exchange(src, dst, send_sem, recv_sem):
         def copy(i):
             device, target = partner(i)
             return pltpu.make_async_remote_copy(
@@ -205,13 +177,6 @@
                 def _():
                     copy(i - WINDOW).wait_send()
 
-                if listen:
-
-                    @pl.when(i % nx == 0)
-                    def _():
-                        _, target = partner(i)
-                        hear(target % nz)
-
                 copy(i).start()
                 return carry
 
@@ -228,7 +193,9 @@
 
         return send, drain
 
-    send, drain = exchange(spread, arrived, a_send, a_recv, True)
+    send, drain = exchange(spread, arrived, a_send, a_recv)
+    hop_out(0, 1)
+    send(0, 8)
 
     vocab = table.shape[1]
     low_count = 256
@@ -256,10 +223,14 @@
     terms = jnp.where(lane == 0, first, jnp.where(lane == 1, second, jnp.where(lane == 2, third, 0.0)))
     wall[mx, mz // STRIDE, mz % STRIDE, :, 3 * part : 3 * part + 128] = terms.astype(BF16)
 
-    begin = jnp.where(mz < STRIDE, 28, 8)
-    send(0, begin)
-    pl.when(above > 0)(lambda: pl.semaphore_wait(ring_hello, above))
-    hop_out(1)
+    def send_hops(at, pace):
+        for q in range(1, up + 1):
+            send(at, at + pace)
+            at += pace
+            hop_in(0, q)
+            if q < up:
+                hop_out(0, q + 1)
+        return at
 
     def send_pieces(stage, at, each, slack):
         for pair in ((0, 1), (2, 3)):
@@ -288,70 +259,75 @@
     column_line = iota((WW, rows), 1) % lines
     for line in range(lines):
         wide[line * WW : (line + 1) * WW, :] = jnp.where(column_line == line, kw_wide, 0.0).astype(BF16)
-    left_over = n - 1 - begin
-
-    def until(share):
-        return begin + left_over * share // 128
-
-    done = begin
-    for q in range(1, up + 1):
-        send(done, until(11 * q))
-        done = until(11 * q)
-        hop_in(q)
-        if q < up:
-            hop_out(q + 1)
-    share = 11 * up
-    for stage in (0, 1):
-        for pair in ((0, 1), (2, 3)):
-            count = group_span(pair[0])[1] - group_span(pair[0])[0]
-            for g in range(count):
-                for k in pair:
-                    piece(stage, k, group_span(k)[0] + g, 1).start()
-                share += 1
-                send(done, until(share))
-                done = until(share)
-            share += 7
-            send(done, until(share))
-            done = until(share)
-            for k in pair:
-                whole(stage, k).wait_recv()
-    send(done, n - 1)
+    at = send_hops(8, 13)
+    at = send_pieces(0, at, 1, 8)
+    at = send_pieces(1, at, 1, 8)
+    send(at, n - 1)
     drain()
 
     quarters = rows // tile
-    ycopies = []
-    for r in range(quarters):
-        here = slice(r * tile, (r + 1) * tile)
-        full = arrived[...].reshape(rows, part)
-        y_own[here, :] = dot(space[here, :], full).astype(BF16)
-        ycopies.append(pltpu.make_async_remote_copy(
+    gathered = wall.reshape(chans, 3 * part + 128)
+    value_weight = gathered.at[:, 0:part]
+    own_rows = pl.ds(pl.multiple_of(core * part, part), part)
+    other_rows = pl.ds(pl.multiple_of((1 - core) * part, part), part)
+    ycopies = [
+        pltpu.make_async_remote_copy(
             src_ref=y_own.at[pl.ds(r * tile, tile)], dst_ref=y_other.at[pl.ds(r * tile, tile)],
             send_sem=y_send.at[r], recv_sem=y_recv.at[r], device_id=other_core, device_id_type=MESH,
-        ))
-        ycopies[-1].start()
-    gathered = wall.reshape(chans, 3 * part + 128)
-    weight = gathered.at[:, 0:part]
-    own_rows = pl.ds(pl.multiple_of(core * part, part), part)
-    other_rows = pl.ds(pl.multiple_of((1 - core) * part, part), part)
-    for r in range(quarters):
+        )
+        for r in range(quarters)
+    ]
+
+    def forward(r):
+        here = slice(r * tile, (r + 1) * tile)
+        y_own[here, :] = dot(space[here, :], arrived[...].reshape(rows, part)).astype(BF16)
+        ycopies[r].start()
+
+    def project(r):
         here = slice(r * tile, (r + 1) * tile)
         ycopies[r].wait_recv()
-        value = dot(y_own[here, :], weight[own_rows, :]) + dot(y_other[here, :], weight[other_rows, :])
+        value = dot(y_own[here, :], value_weight[own_rows, :])
+        value = value + dot(y_other[here, :], value_weight[other_rows, :])
         filt[here, :] = (value * spec[here, :].astype(F32)).astype(BF16)
-    for r in range(quarters):
+
+    def backward(r):
         here = slice(r * tile, (r + 1) * tile)
         got = dot(space[here, :], filt[...]).astype(BF16)
         back[r * per : (r + 1) * per] = got.reshape(per, block, part)
         ycopies[r].wait_send()
+
+    def chain(step):
+        if 0 < step <= up:
+            hop_in(1, step)
+        if step < up:
+            hop_out(1, step + 1)
+        if step == up:
+            whole(2, 0).start()
+            whole(2, 1).start()
+        if step == up + 1:
+            whole(2, 0).wait_recv()
+            whole(2, 1).wait_recv()
+            whole(2, 2).start()
+            whole(2, 3).start()
+
+    work = [functools.partial(f, r) for f in (forward, project, backward) for r in range(quarters)]
+    for at, piece_of_work in enumerate(work):
+        if at % 2 == 0:
+            chain(at // 2)
+        piece_of_work()
     returned[me] = back[me]
-    send, drain = exchange(back, returned, b_send, b_recv, False)
-    at = send_pieces(2, 0, 6, 16)
+    send, drain = exchange(back, returned, b_send, b_recv)
+    send(0, 16)
+    whole(2, 2).wait_recv()
+    whole(2, 3).wait_recv()
+    at = send_pieces(3, 16, 5, 16)
     send(at, n - 1)
-    for q in range(1, up + 1):
-        hop(1, q).wait_send()
-        if q <= down:
-            hop(-1, q).wait_send()
-    for stage in range(3):
+    for stream in range(2):
+        for q in range(1, up + 1):
+            hop(stream, 1, q).wait_send()
+            if q <= down:
+                hop(stream, -1, q).wait_send()
+    for stage in range(4):
         for k in range(4):
             whole(stage, k).wait_send()
 
@@ -435,8 +411,8 @@
             pltpu.VMEM((half, part), BF16), pltpu.VMEM((half, part), BF16),
             pltpu.VMEM((embed_table.shape[1] // 256, 256), F32),
             pltpu.VMEM((rows, rows), BF16), pltpu.VMEM((rows, rows), BF16), pltpu.VMEM((rows, rows), BF16),
-            pltpu.SemaphoreType.REGULAR((nz,)), pltpu.SemaphoreType.REGULAR, dma((n,)), dma((1,)), dma((n,)), dma((1,)),
-            dma((hops,)), dma((hops,)), dma((3, 4)), dma((3, 4)),
+            dma((n,)), dma((1,)), dma((n,)), dma((1,)),
+            dma((2, hops)), dma((2, hops)), dma((4, 4)), dma((4, 4)),
             dma((4,)), dma((4,)), dma, dma, dma((2,)), dma((2,)),
         ],
         compiler_params=pltpu.CompilerParams(

time: 343 us -> 289 us (0.84)
  Pallas kernels: 338 us -> 285 us
    pallas_call x1, Pallas kernels: 338 us -> 285 us  [local(): pl.pallas_call(functools.partial(kernel, nx, nz), out_shape=jax.ShapeDtyp...]
where the time goes in v6:
time: 289 us
  Pallas kernels  285 us (99%)
  other arithmetic  3.59 us (1%)
    pallas_call x1, Pallas kernels, local(): pl.pallas_call(functools.partial(kernel, nx, nz), out_shape=jax.ShapeDtyp...  285 us

profile of v6, /device:TPU:33, one launch (start us, length us, event | category | flops | bytes accessed | tf_op | source)
XLA Modules:
  0.0 288.8 jit_solution(3598345457196685457)
XLA Ops:
  0.7 0.7 compare_select_fusion.emb
  1.3 0.0 copy-start
  1.3 284.5 %shard_map.109 = f32[512,1024]{1,0:T(8,128)} custom-call(bf16[1024,1024]{1,0:T(8,128)(2,1)} %lat.1, bf16[1024,512]{1,0:T(8,128)(2,1)} %bitcast.3, bf16[8,512]{1,0:T(8,128)(2,1)} %wv_in.1, bf16[8,512]{1,0:T(8,128)(2,1)} %wg_in.1, bf16[8,1024]{1,0:T(8,128)(2,1)} %wo_in.1, bf16[4,32768]{1,0:T(4,128)(2,1)} %table.1, s32[1,256]{1,0:T(1,128)} %bitcast.4, ...), custom_call_target="tpu_custom_call" | custom-call | tf_op jit(solution)/shard_map/pallas_call | solution.py:398
  285.9 0.0 copy-done
  285.9 2.9 %add_convert_fusion = bf16[512,1024]{1,0:T(8,128)(2,1)} fusion(f32[512,1024]{1,0:T(8,128)} %shard_map.109, bf16[1024,1024]{1,0:T(8,128)(2,1)S(1)} %copy-done, s32[]{:T(128)S(6)} %select_n.25), kind=kLoop, calls=%fused_computation | loop fusion | flops 1572864 | bytes 4194308 | tf_op jit(solution)/shard_map/convert_element_type | solution.py:426
Async XLA Ops:
  1.3 284.5 %copy-start = (bf16[1024,1024]{1,0:T(8,128)(2,1)S(1)}, bf16[1024,1024]{1,0:T(8,128)(2,1)}, u32[]{:S(2)}) copy-start(bf16[1024,1024]{1,0:T(8,128)(2,1)} %lat.1) | copy-start | bytes 6291460

commit v7 on v6

--- a/solution.py
+++ b/solution.py
@@ -121,24 +121,24 @@
     first_part = pl.ds(0, part)
     later_part = pl.ds(part, 2 * part + 128)
 
-    def hop(stream, direction, q):
+    def hop(direction, q):
         origin = (mz // STRIDE - direction * (q - 1) + groups) % groups
-        ref = wall.at[mx, origin, mz % STRIDE, :, (first_part, later_part)[stream]]
+        ref = wall.at[mx, origin, mz % STRIDE]
         k = (q - 1) if direction > 0 else up + q - 1
         return pltpu.make_async_remote_copy(
-            src_ref=ref, dst_ref=ref, send_sem=s_send.at[stream, k], recv_sem=s_recv.at[stream, k],
+            src_ref=ref, dst_ref=ref, send_sem=s_send.at[k], recv_sem=s_recv.at[k],
             device_id={"sp_1": (mz + direction * STRIDE + nz) % nz}, device_id_type=MESH,
         )
 
-    def hop_in(stream, q):
-        hop(stream, 1, q).wait_recv()
+    def hop_in(q):
+        hop(1, q).wait_recv()
         if q <= down:
-            hop(stream, -1, q).wait_recv()
-
-    def hop_out(stream, q):
-        hop(stream, 1, q).start()
+            hop(-1, q).wait_recv()
+
+    def hop_out(q):
+        hop(1, q).start()
         if q <= down:
-            hop(stream, -1, q).start()
+            hop(-1, q).start()
 
     def group_span(k):
         return ((0, groups), (0, groups), (groups // 2, groups), (0, groups // 2))[k]
@@ -194,7 +194,6 @@
         return send, drain
 
     send, drain = exchange(spread, arrived, a_send, a_recv)
-    hop_out(0, 1)
     send(0, 8)
 
     vocab = table.shape[1]
@@ -222,14 +221,15 @@
     lane = iota((block, 128), 1)
     terms = jnp.where(lane == 0, first, jnp.where(lane == 1, second, jnp.where(lane == 2, third, 0.0)))
     wall[mx, mz // STRIDE, mz % STRIDE, :, 3 * part : 3 * part + 128] = terms.astype(BF16)
+    hop_out(1)
 
     def send_hops(at, pace):
         for q in range(1, up + 1):
             send(at, at + pace)
             at += pace
-            hop_in(0, q)
+            hop_in(q)
             if q < up:
-                hop_out(0, q + 1)
+                hop_out(q + 1)
         return at
 
     def send_pieces(stage, at, each, slack):
@@ -296,24 +296,16 @@
         back[r * per : (r + 1) * per] = got.reshape(per, block, part)
         ycopies[r].wait_send()
 
-    def chain(step):
-        if 0 < step <= up:
-            hop_in(1, step)
-        if step < up:
-            hop_out(1, step + 1)
-        if step == up:
+    work = [functools.partial(f, r) for f in (forward, project, backward) for r in range(quarters)]
+    for at, piece_of_work in enumerate(work):
+        if at == 0:
             whole(2, 0).start()
             whole(2, 1).start()
-        if step == up + 1:
+        if at == 2 * quarters:
             whole(2, 0).wait_recv()
             whole(2, 1).wait_recv()
             whole(2, 2).start()
             whole(2, 3).start()
-
-    work = [functools.partial(f, r) for f in (forward, project, backward) for r in range(quarters)]
-    for at, piece_of_work in enumerate(work):
-        if at % 2 == 0:
-            chain(at // 2)
         piece_of_work()
     returned[me] = back[me]
     send, drain = exchange(back, returned, b_send, b_recv)
@@ -322,11 +314,10 @@
     whole(2, 3).wait_recv()
     at = send_pieces(3, 16, 5, 16)
     send(at, n - 1)
-    for stream in range(2):
-        for q in range(1, up + 1):
-            hop(stream, 1, q).wait_send()
-            if q <= down:
-                hop(stream, -1, q).wait_send()
+    for q in range(1, up + 1):
+        hop(1, q).wait_send()
+        if q <= down:
+            hop(-1, q).wait_send()
     for stage in range(4):
         for k in range(4):
             whole(stage, k).wait_send()
@@ -412,7 +403,7 @@
             pltpu.VMEM((embed_table.shape[1] // 256, 256), F32),
             pltpu.VMEM((rows, rows), BF16), pltpu.VMEM((rows, rows), BF16), pltpu.VMEM((rows, rows), BF16),
             dma((n,)), dma((1,)), dma((n,)), dma((1,)),
-            dma((2, hops)), dma((2, hops)), dma((4, 4)), dma((4, 4)),
+            dma((hops,)), dma((hops,)), dma((4, 4)), dma((4, 4)),
             dma((4,)), dma((4,)), dma, dma, dma((2,)), dma((2,)),
         ],
         compiler_params=pltpu.CompilerParams(

time: 289 us -> 277 us (0.958)
  Pallas kernels: 285 us -> 273 us
    pallas_call x1, Pallas kernels: 285 us -> 273 us  [local(): pl.pallas_call(functools.partial(kernel, nx, nz), out_shape=jax.ShapeDtyp...]
where the time goes in v7:
time: 277 us
  Pallas kernels  273 us (99%)
  other arithmetic  3.59 us (1%)
    pallas_call x1, Pallas kernels, local(): pl.pallas_call(functools.partial(kernel, nx, nz), out_shape=jax.ShapeDtyp...  273 us

profile of v7, /device:TPU:33, one launch (start us, length us, event | category | flops | bytes accessed | tf_op | source)
XLA Modules:
  0.0 277.2 jit_solution(337960087763995548)
XLA Ops:
  0.7 0.7 compare_select_fusion.emb
  1.3 0.0 copy-start
  1.3 272.9 %shard_map.109 = f32[512,1024]{1,0:T(8,128)} custom-call(bf16[1024,1024]{1,0:T(8,128)(2,1)} %lat.1, bf16[1024,512]{1,0:T(8,128)(2,1)} %bitcast.3, bf16[8,512]{1,0:T(8,128)(2,1)} %wv_in.1, bf16[8,512]{1,0:T(8,128)(2,1)} %wg_in.1, bf16[8,1024]{1,0:T(8,128)(2,1)} %wo_in.1, bf16[4,32768]{1,0:T(4,128)(2,1)} %table.1, s32[1,256]{1,0:T(1,128)} %bitcast.4, ...), custom_call_target="tpu_custom_call" | custom-call | tf_op jit(solution)/shard_map/pallas_call | solution.py:389
  274.2 0.0 copy-done
  274.3 2.9 %add_convert_fusion = bf16[512,1024]{1,0:T(8,128)(2,1)} fusion(f32[512,1024]{1,0:T(8,128)} %shard_map.109, bf16[1024,1024]{1,0:T(8,128)(2,1)S(1)} %copy-done, s32[]{:T(128)S(6)} %select_n.25), kind=kLoop, calls=%fused_computation | loop fusion | flops 1572864 | bytes 4194308 | tf_op jit(solution)/shard_map/convert_element_type | solution.py:417
Async XLA Ops:
  1.3 272.9 %copy-start = (bf16[1024,1024]{1,0:T(8,128)(2,1)S(1)}, bf16[1024,1024]{1,0:T(8,128)(2,1)}, u32[]{:S(2)}) copy-start(bf16[1024,1024]{1,0:T(8,128)(2,1)} %lat.1) | copy-start | bytes 6291460

commit v8 on v7

--- a/solution.py
+++ b/solution.py
@@ -57,7 +57,7 @@
     nx, nz,
     lat, spec, wv_in, wg_in, wo_in, table, ids, emb, kw, kh, kt,
     out,
-    spread, arrived, spin, spout, back, returned, y_own, y_other, filt, gain,
+    spread, arrived, spin, spout, back, returned, y_own, y_other, filt, gain, total,
     wall, wo_other, mix_own, mix_other, counts, space, wide, narrow,
     a_send, a_recv, b_send, b_recv, s_send, s_recv, r_send, r_recv,
     y_send, y_recv, o_send, o_recv, m_send, m_recv,
@@ -70,14 +70,24 @@
     mx, mz, core = lax.axis_index("sp_0"), lax.axis_index("sp_1"), lax.axis_index("ch")
     me = mx * nz + mz
     other_core = {"ch": 1 - core}
+    tile = rows // nx
+    per = tile // block
+
+    def x_step(turn):
+        return jnp.where(turn == 0, 2, jnp.where(turn == 1, 1, jnp.where(turn == 2, 3, 0)))
 
     def partner(i):
-        j = n - 1 - i
-        zi, dx = j // nx, j % nx
+        zi = nz - 1 - i % nz
         m = (zi + 1) // 2
         dz = jnp.where(zi % 2 == 1, m, nz - m) % nz
-        tx, tz = (mx + dx) % nx, (mz + dz) % nz
+        tx, tz = (mx + x_step(i // nz)) % nx, (mz + dz) % nz
         return {"sp_0": tx, "sp_1": tz}, tx * nz + tz
+
+    def blocks_of(column):
+        return pl.ds(pl.multiple_of(column * nz, nz), nz)
+
+    def rows_of(column):
+        return pl.ds(pl.multiple_of(column * tile, tile), tile)
 
     barrier = pltpu.get_barrier_semaphore()
 
@@ -97,8 +107,6 @@
             line_of == line, spread_rows, jnp.zeros_like(spread_rows)
         )
     mine = pl.ds(pl.multiple_of(core * part, 128), part)
-    tile = 256
-    per = tile // block
 
     def widen(r, carry):
         at = pl.ds(pl.multiple_of(r * tile, tile), tile)
@@ -167,7 +175,7 @@
             device, target = partner(i)
             return pltpu.make_async_remote_copy(
                 src_ref=src.at[target], dst_ref=dst.at[me],
-                send_sem=send_sem.at[i], recv_sem=recv_sem.at[0],
+                send_sem=send_sem.at[i], recv_sem=recv_sem.at[i // nz],
                 device_id=device, device_id_type=MESH,
             )
 
@@ -188,12 +196,16 @@
                 return carry
 
             lax.fori_loop(n - 1 - WINDOW, n - 1, body, 0)
-            some = dst.at[pl.ds(0, n - 1)]
-            pltpu.make_async_copy(some, some, recv_sem.at[0]).wait()
-
-        return send, drain
-
-    send, drain = exchange(spread, arrived, a_send, a_recv)
+
+        def arrive(turn):
+            column = (mx - (2, 1, 3, 0)[turn] + nx) % nx
+            some = dst.at[pl.ds(column * nz, nz - 1 if turn == nx - 1 else nz)]
+            pltpu.make_async_copy(some, some, recv_sem.at[turn]).wait()
+            return column
+
+        return send, drain, arrive
+
+    send, drain, arrive = exchange(spread, arrived, a_send, a_recv)
     send(0, 8)
 
     vocab = table.shape[1]
@@ -211,8 +223,8 @@
         return total + piece.astype(F32) * counts[pl.ds(h, 1), :]
 
     few = table.shape[0]
-    total = lax.fori_loop(0, high_count, tally, jnp.zeros((few, low_count), F32))
-    pooled4 = jnp.sum(total, axis=1, keepdims=True) * (1.0 / prompt)
+    tallied = lax.fori_loop(0, high_count, tally, jnp.zeros((few, low_count), F32))
+    pooled4 = jnp.sum(tallied, axis=1, keepdims=True) * (1.0 / prompt)
     pooled8 = jnp.concatenate([pooled4] * (block // few), axis=0)
     pooled8 = jnp.where(iota((block, 1), 0) // few == core, pooled8, 0.0)
     first = pooled8.astype(BF16).astype(F32)
@@ -263,7 +275,14 @@
     at = send_pieces(0, at, 1, 8)
     at = send_pieces(1, at, 1, 8)
     send(at, n - 1)
+    for turn in range(nx - 1):
+        column = arrive(turn)
+        for r in range(nx):
+            here = slice(r * tile, (r + 1) * tile)
+            got = dot(space[here, rows_of(column)], arrived[blocks_of(column)].reshape(tile, part))
+            total[here, :] = got if turn == 0 else total[here, :] + got
     drain()
+    column = arrive(nx - 1)
 
     quarters = rows // tile
     gathered = wall.reshape(chans, 3 * part + 128)
@@ -280,7 +299,8 @@
 
     def forward(r):
         here = slice(r * tile, (r + 1) * tile)
-        y_own[here, :] = dot(space[here, :], arrived[...].reshape(rows, part)).astype(BF16)
+        got = dot(space[here, rows_of(column)], arrived[blocks_of(column)].reshape(tile, part))
+        y_own[here, :] = (total[here, :] + got).astype(BF16)
         ycopies[r].start()
 
     def project(r):
@@ -290,29 +310,34 @@
         value = value + dot(y_other[here, :], value_weight[other_rows, :])
         filt[here, :] = (value * spec[here, :].astype(F32)).astype(BF16)
 
-    def backward(r):
-        here = slice(r * tile, (r + 1) * tile)
-        got = dot(space[here, :], filt[...]).astype(BF16)
-        back[r * per : (r + 1) * per] = got.reshape(per, block, part)
+    def backward(turn):
+        target = (mx + (2, 1, 3, 0)[turn]) % nx
+        got = dot(space[rows_of(target), :], filt[...]).astype(BF16)
+        back[blocks_of(target)] = got.reshape(per, block, part)
+
+    whole(2, 0).start()
+    whole(2, 1).start()
+    for r in range(nx):
+        forward(r)
+    for r in range(nx):
+        project(r)
+    whole(2, 0).wait_recv()
+    whole(2, 1).wait_recv()
+    whole(2, 2).start()
+    whole(2, 3).start()
+    send, drain, arrive = exchange(back, returned, b_send, b_recv)
+    backward(0)
+    send(0, nz // 2)
+    backward(1)
+    send(nz // 2, nz)
+    for turn in range(2, nx):
+        backward(turn)
+    returned[me] = back[me]
+    for r in range(nx):
         ycopies[r].wait_send()
-
-    work = [functools.partial(f, r) for f in (forward, project, backward) for r in range(quarters)]
-    for at, piece_of_work in enumerate(work):
-        if at == 0:
-            whole(2, 0).start()
-            whole(2, 1).start()
-        if at == 2 * quarters:
-            whole(2, 0).wait_recv()
-            whole(2, 1).wait_recv()
-            whole(2, 2).start()
-            whole(2, 3).start()
-        piece_of_work()
-    returned[me] = back[me]
-    send, drain = exchange(back, returned, b_send, b_recv)
-    send(0, 16)
     whole(2, 2).wait_recv()
     whole(2, 3).wait_recv()
-    at = send_pieces(3, 16, 5, 16)
+    at = send_pieces(3, nz, 4, 16)
     send(at, n - 1)
     for q in range(1, up + 1):
         hop(1, q).wait_send()
@@ -342,13 +367,21 @@
         return carry
 
     lax.fori_loop(0, quarters, gate, 0)
+    for turn in range(nx - 1):
+        column = arrive(turn)
+        for r in range(nx):
+            here = slice(r * tile, (r + 1) * tile)
+            got = dot(wide[here, rows_of(column)], returned[blocks_of(column)].reshape(tile, part))
+            total[here, :] = got if turn == 0 else total[here, :] + got
     drain()
+    last = arrive(nx - 1)
 
     half = rows // 2
 
     def finish(r, dst, base):
         here = pl.ds(pl.multiple_of(base + r * tile, tile), tile)
-        mix = dot(wide[here, :], returned[...].reshape(rows, part)) * gain[here, :]
+        mix = dot(wide[here, rows_of(last)], returned[blocks_of(last)].reshape(tile, part))
+        mix = (total[here, :] + mix) * gain[here, :]
         dst[pl.ds(pl.multiple_of(r * tile, tile), tile), :] = mix.astype(BF16)
 
     mcopies = []
@@ -396,13 +429,13 @@
             pltpu.VMEM((8, 128), BF16), pltpu.VMEM((half, part), BF16),
             exchanged, exchanged,
             plain, plain, plain,
-            pltpu.VMEM((rows, part), F32),
+            pltpu.VMEM((rows, part), F32), pltpu.VMEM((rows, part), F32),
             pltpu.VMEM((nx, groups, STRIDE, block, 3 * part + 128), BF16),
             pltpu.VMEM((nx, groups, STRIDE, block, part + 128), BF16),
             pltpu.VMEM((half, part), BF16), pltpu.VMEM((half, part), BF16),
             pltpu.VMEM((embed_table.shape[1] // 256, 256), F32),
             pltpu.VMEM((rows, rows), BF16), pltpu.VMEM((rows, rows), BF16), pltpu.VMEM((rows, rows), BF16),
-            dma((n,)), dma((1,)), dma((n,)), dma((1,)),
+            dma((n,)), dma((nx,)), dma((n,)), dma((nx,)),
             dma((hops,)), dma((hops,)), dma((4, 4)), dma((4, 4)),
             dma((4,)), dma((4,)), dma, dma, dma((2,)), dma((2,)),
         ],

time: 277 us -> 276 us (level)
  no operation moved by 1% of the time
where the time goes in v8:
time: 276 us; the launch traced here: 275 us
  Pallas kernels  271 us (98%)
  other arithmetic  3.59 us (1%)
    pallas_call x1, Pallas kernels, local(): pl.pallas_call(functools.partial(kernel, nx, nz), out_shape=jax.ShapeDtyp...  271 us

profile of v8, /device:TPU:33, one launch (start us, length us, event | category | flops | bytes accessed | tf_op | source)
XLA Modules:
  0.0 275.2 jit_solution(11127071378304431375)
XLA Ops:
  0.7 0.7 compare_select_fusion.emb
  1.3 0.0 copy-start
  1.3 270.9 %shard_map.109 = f32[512,1024]{1,0:T(8,128)} custom-call(bf16[1024,1024]{1,0:T(8,128)(2,1)} %lat.1, bf16[1024,512]{1,0:T(8,128)(2,1)} %bitcast.3, bf16[8,512]{1,0:T(8,128)(2,1)} %wv_in.1, bf16[8,512]{1,0:T(8,128)(2,1)} %wg_in.1, bf16[8,1024]{1,0:T(8,128)(2,1)} %wo_in.1, bf16[4,32768]{1,0:T(4,128)(2,1)} %table.1, s32[1,256]{1,0:T(1,128)} %bitcast.4, ...), custom_call_target="tpu_custom_call" | custom-call | tf_op jit(solution)/shard_map/pallas_call | solution.py:422
  272.3 0.0 copy-done
  272.3 2.9 %add_convert_fusion = bf16[512,1024]{1,0:T(8,128)(2,1)} fusion(f32[512,1024]{1,0:T(8,128)} %shard_map.109, bf16[1024,1024]{1,0:T(8,128)(2,1)S(1)} %copy-done, s32[]{:T(128)S(6)} %select_n.25), kind=kLoop, calls=%fused_computation | loop fusion | flops 1572864 | bytes 4194308 | tf_op jit(solution)/shard_map/convert_element_type | solution.py:450
Async XLA Ops:
  1.3 270.9 %copy-start = (bf16[1024,1024]{1,0:T(8,128)(2,1)S(1)}, bf16[1024,1024]{1,0:T(8,128)(2,1)}, u32[]{:S(2)}) copy-start(bf16[1024,1024]{1,0:T(8,128)(2,1)} %lat.1) | copy-start | bytes 6291460

commit v9 on v8

--- a/solution.py
+++ b/solution.py
@@ -21,7 +21,7 @@
 BF16 = jnp.bfloat16
 MESH = pl.DeviceIdType.MESH
 STRIDE = 4
-WINDOW = 40
+WINDOW = 64
 
 
 def cas_table(length):
@@ -399,10 +399,12 @@
     for r in range(half // tile):
         here = slice(r * tile, (r + 1) * tile)
         mcopies[r].wait()
+        own_cells = pl.ds(pl.multiple_of(core * half + r * tile, tile), tile)
         for at, weight in ((left, gathered.at[:, 2 * part : 3 * part]), (right, others.at[:, 0:part])):
-            out[here, at] = dot(mix_own[here, :], weight[own_rows, :]) + dot(
+            added = dot(mix_own[here, :], weight[own_rows, :]) + dot(
                 mix_other[here, :], weight[other_rows, :]
             )
+            out[here, at] = (lat[own_cells, at].astype(F32) + added).astype(BF16)
 
 
 def local(nx, nz, latents, spectrum, w_value, w_gate, w_out, embed_table, prompt_ids, noise_step):
@@ -419,9 +421,9 @@
     dma = pltpu.SemaphoreType.DMA
     exchanged = pltpu.VMEM((n, rows // n, part), BF16)
     plain = pltpu.VMEM((rows, part), BF16)
-    summed = pl.pallas_call(
+    return pl.pallas_call(
         functools.partial(kernel, nx, nz),
-        out_shape=jax.ShapeDtypeStruct((half, chans), F32),
+        out_shape=jax.ShapeDtypeStruct((half, chans), BF16),
         in_specs=[vmem] * 11,
         out_specs=vmem,
         scratch_shapes=[
@@ -446,8 +448,6 @@
         latents, spectrum.reshape(rows, part), w_value, w_gate, w_out, embed_table,
         prompt_ids.reshape(1, -1), emb, cas_table(WW), cas_table(HH), cas_table(TT),
     )
-    residual = lax.dynamic_slice_in_dim(latents, core * half, half, 0)
-    return (residual.astype(F32) + summed).astype(BF16)
 
 
 def solution(mesh):

time: 276 us -> 275 us (level)
  other arithmetic: 3.59 us -> 0.67 us
    convert_element_type x1 -> x0, other arithmetic: 2.92 us -> none  [local(): return (residual.astype(F32) + summed).astype(BF16)]
where the time goes in v9:
time: 275 us
  Pallas kernels  272 us (99%)
    pallas_call x1, Pallas kernels, local(): pl.pallas_call(functools.partial(kernel, nx, nz), out_shape=jax.ShapeDtyp...  272 us

profile of v9, /device:TPU:33, one launch (start us, length us, event | category | flops | bytes accessed | tf_op | source)
XLA Modules:
  0.0 275.2 jit_solution(14275623524231960622)
XLA Ops:
  0.7 0.7 compare_select_fusion.emb
  1.3 271.6 %shard_map.109 = bf16[512,1024]{1,0:T(8,128)(2,1)} custom-call(bf16[1024,1024]{1,0:T(8,128)(2,1)} %lat.1, bf16[1024,512]{1,0:T(8,128)(2,1)} %bitcast.3, bf16[8,512]{1,0:T(8,128)(2,1)} %wv_in.1, bf16[8,512]{1,0:T(8,128)(2,1)} %wg_in.1, bf16[8,1024]{1,0:T(8,128)(2,1)} %wo_in.1, bf16[4,32768]{1,0:T(4,128)(2,1)} %table.1, s32[1,256]{1,0:T(1,128)} %bitcast.4, ...), custom_call_target="tpu_custom_call" | custom-call | tf_op jit(solution)/shard_map/pallas_call | solution.py:424
  272.9 2.3 copy.14

commit v10 on v9

--- a/solution.py
+++ b/solution.py
@@ -21,7 +21,7 @@
 BF16 = jnp.bfloat16
 MESH = pl.DeviceIdType.MESH
 STRIDE = 4
-WINDOW = 64
+WINDOW = 96
 
 
 def cas_table(length):

time: 275 us -> 276 us (level)
  no operation moved by 1% of the time
where the time goes in v10:
time: 276 us
  Pallas kernels  272 us (99%)
    pallas_call x1, Pallas kernels, local(): pl.pallas_call(functools.partial(kernel, nx, nz), out_shape=jax.ShapeDtyp...  272 us

profile of v10, /device:TPU:33, one launch (start us, length us, event | category | flops | bytes accessed | tf_op | source)
XLA Modules:
  0.0 275.5 jit_solution(14224591755236190898)
XLA Ops:
  0.7 0.7 compare_select_fusion.emb
  1.3 272.0 %shard_map.109 = bf16[512,1024]{1,0:T(8,128)(2,1)} custom-call(bf16[1024,1024]{1,0:T(8,128)(2,1)} %lat.1, bf16[1024,512]{1,0:T(8,128)(2,1)} %bitcast.3, bf16[8,512]{1,0:T(8,128)(2,1)} %wv_in.1, bf16[8,512]{1,0:T(8,128)(2,1)} %wg_in.1, bf16[8,1024]{1,0:T(8,128)(2,1)} %wo_in.1, bf16[4,32768]{1,0:T(4,128)(2,1)} %table.1, s32[1,256]{1,0:T(1,128)} %bitcast.4, ...), custom_call_target="tpu_custom_call" | custom-call | tf_op jit(solution)/shard_map/pallas_call | solution.py:424
  273.3 2.3 copy.14
